TPU v7x, 256 devices: a whole 4x4x8 slice. The times are simulated.
256 devices in a mesh: dev: 256 (over x, y, z, core).
Axes of the slice: x: 4, y: 4, z: 8, core: 2. Of those that a mesh axis runs over, the one named last changes fastest.
Arguments:
- field: float32 [16, 16, 16, 32768], P(None, None, None, 'dev'), may hold values from -6 to 6
- s_mats: float32 [3, 18, 18], replicated, may hold values from -1.5 to 1.5
- lam: float32 [3, 18], replicated, may hold values from 0.2 to 4
- coeff: float32 [3, 32768], P(None, 'dev'), may hold values from 0.5 to 2
- nbr_src: int32 [6, 32768], P(None, 'dev'), may hold values from 0 to 7, as said below
- nbr_idx: int32 [6, 32768], P(None, 'dev'), may hold values from 0 to 767, as said below
- orient: int32 [6, 32768], P(None, 'dev'), may hold values from 0 to 3, as said below
- send_x: int32 [2, 4096], P(None, 'dev'), may hold values from 0 to 255, as said below
- send_y: int32 [2, 4096], P(None, 'dev'), may hold values from 256 to 511, as said below
- send_z: int32 [2, 16384], P(None, 'dev'), may hold values from 512 to 767, as said below
Outputs:
- smoothed: float32 [16, 16, 16, 32768], P(None, None, None, 'dev')
Inputs may be any that keep to these rules, and one draw needn't show every extreme that they name: `nbr_src`: 0 where the face lies on the boundary of the box of elements, 1 where the element across it is on the same device, 2 + j where it is on the device whose index is lower by o_j. Devices form a 4 x 4 x 16 grid, first index fastest; each holds a 8 x 8 x 2 block of the box, its elements in slots in any order and each stored mirrored or not along each of its three axes. Every face not on the boundary is shared by exactly two elements and listed from both sides. `nbr_idx`: for code 1 the id g * 128 + s of the face g of the element in slot s that meets this face; for code 2 + j a position in list j of the sending device; 0 for code 0. `orient`: the two sides of a shared face carry the same code; 0 on the boundary. `send_x`: row r (list r) holds the ids of the 16 faces of this device's block on its low (r = 0) or high (r = 1) side across the first dimension, each once, ordered by the faces' block coordinates along the second dimension, then the third; the device whose index is higher by o_r reads it. Each id is that of face 0 or 1 of its element. `send_y`: as send_x, across the second dimension (lists 2 and 3), 16 faces ordered by the first block coordinate, then the third; each id is that of face 2 or 3 of its element. `send_z`: as send_x, across the third dimension (lists 4 and 5), 64 faces ordered by the first block coordinate, then the second; each id is that of face 4 or 5 of its element.
All inputs are finite; a program needn't handle non-finite values.
Results may differ from a plain program's by a relative error of at most 0.0003.
Values sent between devices are 32-bit elements; how exact they have to be, the bound alone decides.
No kernel may reach another device: no remote copies, remote signals or barrier semaphores. Data moves between devices by JAX's collectives and lax.ppermute only.
A program may use at most 128 MiB of HBM per device.

v0:
```python
import functools

import jax
import jax.numpy as jnp
from jax import lax
from jax.experimental import pallas as pl
from jax.experimental.pallas import tpu as pltpu
from jax.sharding import PartitionSpec as P

DEV_X = 4
DEV_Y = 4
OFFSETS = (-1, 1, -DEV_X, DEV_X, -DEV_X * DEV_Y, DEV_X * DEV_Y)
NP = 16
NE = 18
PLANE = NP * NP
LANES = 128
WIDE = 336
NARROW = PLANE + 4 * NP
CHUNK = 8
DEEP = NE * CHUNK
F32 = jnp.float32
BF16 = jnp.bfloat16


def neighbour_pairs(direction, size):
    axis = direction // 2
    step = 1 if direction % 2 else -1
    layout = (DEV_X, DEV_Y, size // (DEV_X * DEV_Y))
    pairs = []
    for i in range(size):
        place = (i % DEV_X, i // DEV_X % DEV_Y, i // (DEV_X * DEV_Y))
        if 0 <= place[axis] + step < layout[axis]:
            pairs.append((i, i + OFFSETS[direction]))
    return pairs


def lane_take(values, index):
    return jnp.take_along_axis(values, index, axis=1, mode="promise_in_bounds")


def lanes(shape):
    return lax.broadcasted_iota(jnp.int32, shape, 1)


def pack_axis(axis, plane, table, low_ref, high_ref):
    count = table.shape[1]
    blocks = LANES // count
    rows = PLANE // blocks
    low, high = table[0:1], table[1:2]
    forward = jnp.concatenate([low, high] * (blocks // 2), axis=1)
    backward = jnp.concatenate([high, low] * (blocks // 2), axis=1)
    patterns = []
    for ids in (forward, backward):
        ids = jnp.broadcast_to(ids, (8, LANES))
        patterns.append((ids & (LANES - 1), (ids // LANES) == 2 * axis + 1))
    lane_block = lanes((8, LANES)) // count
    for row in range(0, rows, 8):
        low_value = jnp.zeros((8, LANES), F32)
        high_value = jnp.zeros((8, LANES), F32)
        for block in range(blocks):
            slot, is_high = patterns[block % 2]
            start = block * rows + row
            got = jnp.where(is_high, lane_take(plane(1, start), slot), lane_take(plane(0, start), slot))
            low_value = jnp.where(lane_block == block, got, low_value)
            high_value = jnp.where(lane_block == block ^ 1, got, high_value)
        low_ref[row : row + 8] = low_value
        high_ref[row : row + 8] = high_value


def unpack_face(face, plane, low_ref, high_ref, source, index, code, put):
    axis = face // 2
    rows = low_ref.shape[0]
    blocks = PLANE // rows
    count = LANES // blocks
    full = lambda row: jnp.broadcast_to(row, (8, LANES))
    source, index, code = full(source), full(index), full(code)
    slot = index & (LANES - 1)
    local_high = (source == 1) & ((index // LANES) == 2 * axis + 1)
    local = source == 1
    from_low = source == 2 + 2 * axis
    from_high = source == 3 + 2 * axis
    position = index & (count - 1)
    flip_first = (code & 1) == 1
    flip_second = (code & 2) == 2
    reverse = 7 - lax.broadcasted_iota(jnp.int32, (8, LANES), 0)

    def fetch(start):
        block, row = start // rows, start % rows
        here = jnp.where(local_high, lane_take(plane(1, start), slot), lane_take(plane(0, start), slot))
        low = lane_take(low_ref[row : row + 8], position + block * count)
        high = lane_take(high_ref[row : row + 8], position + (block ^ 1) * count)
        away = jnp.where(from_low, low, jnp.where(from_high, high, 0.0))
        return jnp.where(local, here, away)

    def turn(value):
        return jnp.take_along_axis(value, reverse, axis=0, mode="promise_in_bounds")

    for p in range(NP // 2):
        q = NP - 1 - p
        pieces = [[fetch(line * NP), fetch(line * NP + 8)] for line in (p, q)]
        for line, near, far in ((p, pieces[0], pieces[1]), (q, pieces[1], pieces[0])):
            first = [jnp.where(flip_first, far[h], near[h]) for h in range(2)]
            put(line, [jnp.where(flip_second, turn(first[1 - h]), first[h]) for h in range(2)])


def field_plane(field_ref, axis):
    def plane(side, start):
        layer = 1 if side == 0 else NP - 2
        if axis == 0:
            return field_ref[layer * PLANE + start : layer * PLANE + start + 8]
        if axis == 1:
            base = (start // NP) * PLANE + layer * NP + start % NP
            return field_ref[base : base + 8]
        return field_ref[pl.ds(start * NP + layer, 8, stride=NP)]

    return plane


def rim_plane(rim_ref, axis):
    def plane(side, start):
        base = (2 * axis + side) * PLANE + start
        return rim_ref[base : base + 8]

    return plane


def pack_kernel(field_ref, sx_ref, sy_ref, sz_ref, *out_refs):
    for axis, table_ref in enumerate((sx_ref, sy_ref, sz_ref)):
        pack_axis(axis, field_plane(field_ref, axis), table_ref[...], out_refs[2 * axis], out_refs[2 * axis + 1])


def split(value):
    high = value.astype(BF16)
    return high, (value - high.astype(F32)).astype(BF16)


def stacked(value):
    high, low = split(value)
    return jnp.concatenate([high, high, low], axis=0)


def operator(value):
    high, low = split(value)
    return jnp.concatenate([high, low, high], axis=1)


def exact_dot(a, b):
    return jnp.dot(a, b, precision=lax.Precision.HIGHEST, preferred_element_type=F32)


def operators_kernel(s_ref, lam_ref, coeff_ref, main_ref, rim_ref, back_ref, to_ref, from_ref, base_ref):
    iota = lambda shape, dim: lax.broadcasted_iota(jnp.int32, shape, dim)

    def node(kidx, small_first):
        inner = kidx < PLANE
        t = kidx - PLANE
        group = t // NP
        along = 1 + t % NP
        if small_first:
            return jnp.where(inner, 1 + kidx // NP, jnp.where(group == 0, 0, jnp.where(group == 1, NE - 1, along)))
        return jnp.where(inner, 1 + kidx % NP, jnp.where(group == 2, 0, jnp.where(group == 3, NE - 1, along)))

    def hot(cond):
        return jnp.where(cond, 1.0, 0.0).astype(F32)

    wide_b = hot(iota((WIDE, NE), 0) // NE == iota((WIDE, NE), 1))
    wide_c = hot((iota((WIDE, NE), 0) % NE == iota((WIDE, NE), 1)) & (iota((WIDE, NE), 0) < NE * NE))
    wide_bt = hot(iota((NE, WIDE), 1) // NE == iota((NE, WIDE), 0))
    wide_ct = hot((iota((NE, WIDE), 1) % NE == iota((NE, WIDE), 0)) & (iota((NE, WIDE), 1) < NE * NE))
    node_j = hot(node(iota((NARROW, NE), 0), True) == iota((NARROW, NE), 1))
    node_k = hot(node(iota((NARROW, NE), 0), False) == iota((NARROW, NE), 1))
    node_jt = hot(node(iota((NE, NARROW), 1), True) == iota((NE, NARROW), 0))
    node_kt = hot(node(iota((NE, NARROW), 1), False) == iota((NE, NARROW), 0))
    s0, s1, s2 = s_ref[0], s_ref[1], s_ref[2]
    t0, t1, t2 = s0.T, s1.T, s2.T
    ahead = exact_dot(wide_b, exact_dot(t1, node_jt)) * exact_dot(wide_c, exact_dot(t2, node_kt))
    main_ref[...] = operator(ahead[:, :PLANE])
    rim_ref[...] = operator(ahead[:, PLANE:])
    back = exact_dot(node_j, exact_dot(s1, wide_bt)) * exact_dot(node_k, exact_dot(s2, wide_ct))
    back_ref[...] = operator(back)
    deep = hot(iota((DEEP, NE), 0) // CHUNK == iota((DEEP, NE), 1))
    deep_t = hot(iota((NE, DEEP), 1) // CHUNK == iota((NE, DEEP), 0))
    same = hot(iota((DEEP, DEEP), 0) % CHUNK == iota((DEEP, DEEP), 1) % CHUNK)
    to_ref[...] = operator(exact_dot(deep, exact_dot(t0, deep_t)) * same)
    from_ref[...] = operator(exact_dot(deep, exact_dot(s0, deep_t)) * same)
    col_b = jnp.sum(wide_b * lam_ref[1:2], axis=1, keepdims=True)
    col_c = jnp.sum(wide_c * lam_ref[2:3], axis=1, keepdims=True)
    base_ref[...] = col_b * coeff_ref[1:2] + col_c * coeff_ref[2:3]


def mm(a, b):
    return jnp.dot(a, b, preferred_element_type=F32)


def solve_kernel(
    field_ref, src_ref, idx_ref, code_ref, sx_ref, sy_ref, sz_ref, lam_ref, coeff_ref,
    main_ref, rim_op_ref, back_ref, to_ref, from_ref, base_ref,
    m0, m1, m2, m3, m4, m5,
    inner_ref, rim_ref, o0, o1, o2, o3, o4, o5,
    ghost_ref, work_ref,
):
    messages = (m0, m1, m2, m3, m4, m5)
    outs = (o0, o1, o2, o3, o4, o5)
    for face in range(6):
        axis = face // 2

        def put(line, pieces, face=face):
            for h in range(2):
                ghost_ref[pl.ds(face * PLANE + line * NP + 8 * h, 8)] = pieces[h]

        unpack_face(
            face, field_plane(field_ref, axis), messages[2 * axis], messages[2 * axis + 1],
            src_ref[face : face + 1], idx_ref[face : face + 1], code_ref[face : face + 1], put,
        )

    both = lambda load: jnp.concatenate([load(0), load(1)], axis=1)
    for pair in range(NP // 2):
        i = lambda s: 2 * pair + s
        inside = both(lambda s: field_ref[i(s) * PLANE : (i(s) + 1) * PLANE])
        edge = jnp.concatenate(
            [both(lambda s: ghost_ref[f * PLANE + i(s) * NP : f * PLANE + (i(s) + 1) * NP]) for f in range(2, 6)], axis=0
        )
        got = mm(main_ref[...], stacked(inside)) + mm(rim_op_ref[...], stacked(edge))
        for s in range(2):
            work_ref[1 + i(s)] = got[:, s * LANES : (s + 1) * LANES]
    got = mm(main_ref[...], stacked(both(lambda s: ghost_ref[s * PLANE : (s + 1) * PLANE])))
    work_ref[0] = got[:, :LANES]
    work_ref[NE - 1] = got[:, LANES:]

    scale = coeff_ref[0:1]

    def middle(step):
        rows = [pl.ds(pl.multiple_of((2 * step + s) * CHUNK, CHUNK), CHUNK) for s in range(2)]
        chunk = both(lambda s: work_ref[:, rows[s], :].reshape(DEEP, LANES))
        coef = mm(to_ref[...], stacked(chunk))
        divisor = both(
            lambda s: jnp.concatenate([lam_ref[0, a] * scale + base_ref[rows[s], :] for a in range(NE)], axis=0)
        )
        solved = mm(from_ref[...], stacked(coef / divisor))
        for s in range(2):
            work_ref[:, rows[s], :] = solved[:, s * LANES : (s + 1) * LANES].reshape(NE, CHUNK, LANES)

    for step in range(WIDE // CHUNK // 2):
        middle(step)

    got = mm(back_ref[:PLANE], stacked(both(lambda s: work_ref[s * (NE - 1)])))
    rim_ref[0:PLANE] = got[:, :LANES]
    rim_ref[PLANE : 2 * PLANE] = got[:, LANES:]
    for pair in range(NP // 2):
        got = mm(back_ref[...], stacked(both(lambda s: work_ref[1 + 2 * pair + s])))
        for s in range(2):
            i = 2 * pair + s
            part = got[:, s * LANES : (s + 1) * LANES]
            inner_ref[i * PLANE : (i + 1) * PLANE] = part[:PLANE]
            for f in range(2, 6):
                start = PLANE + (f - 2) * NP
                rim_ref[f * PLANE + i * NP : f * PLANE + (i + 1) * NP] = part[start : start + NP]
    for axis, table_ref in enumerate((sx_ref, sy_ref, sz_ref)):
        pack_axis(axis, rim_plane(rim_ref, axis), table_ref[...], outs[2 * axis], outs[2 * axis + 1])


def finish_kernel(inner_ref, rim_ref, src_ref, idx_ref, code_ref, m0, m1, m2, m3, m4, m5, out_ref):
    messages = (m0, m1, m2, m3, m4, m5)
    out_ref[...] = inner_ref[...]
    for face in range(6):
        axis = face // 2
        layer = 1 if face % 2 == 0 else NP - 2

        def put(line, pieces, axis=axis, layer=layer):
            for h in range(2):
                if axis == 0:
                    place = pl.ds(layer * PLANE + line * NP + 8 * h, 8)
                elif axis == 1:
                    place = pl.ds(line * PLANE + layer * NP + 8 * h, 8)
                else:
                    place = pl.ds((line * NP + 8 * h) * NP + layer, 8, stride=NP)
                out_ref[place] = out_ref[place] + pieces[h]

        unpack_face(
            face, rim_plane(rim_ref, axis), messages[2 * axis], messages[2 * axis + 1],
            src_ref[face : face + 1], idx_ref[face : face + 1], code_ref[face : face + 1], put,
        )


VMEM = pl.BlockSpec(memory_space=pltpu.VMEM)
SMEM = pl.BlockSpec(memory_space=pltpu.SMEM)


def message_shapes(tables):
    shapes = []
    for table in tables:
        rows = PLANE * table.shape[1] // LANES
        shapes += [jax.ShapeDtypeStruct((rows, LANES), F32)] * 2
    return shapes


def exchange(messages):
    arrived = []
    for direction in range(6):
        pairs = neighbour_pairs(direction, lax.axis_size("dev"))
        arrived.append(lax.ppermute(messages[direction], "dev", pairs))
    return arrived


def shards(field, s_mats, lam, coeff, nbr_src, nbr_idx, orient, send_x, send_y, send_z):
    flat = field.reshape(NP * PLANE, LANES)
    tables = (send_x, send_y, send_z)
    shape = jax.ShapeDtypeStruct
    outgoing = pl.pallas_call(
        pack_kernel, out_shape=message_shapes(tables), in_specs=[VMEM] * 4, out_specs=[VMEM] * 6, name="pack",
    )(flat, *tables)
    arrived = exchange(outgoing)
    operators = pl.pallas_call(
        operators_kernel,
        out_shape=[
            shape((WIDE, 3 * PLANE), BF16), shape((WIDE, 12 * NP), BF16), shape((NARROW, 3 * WIDE), BF16),
            shape((DEEP, 3 * DEEP), BF16), shape((DEEP, 3 * DEEP), BF16), shape((WIDE, LANES), F32),
        ],
        in_specs=[VMEM] * 3, out_specs=[VMEM] * 6, name="operators",
    )(s_mats, lam, coeff)
    solved = pl.pallas_call(
        solve_kernel,
        out_shape=[shape((NP * PLANE, LANES), F32), shape((6 * PLANE, LANES), F32)] + message_shapes(tables),
        in_specs=[VMEM] * 7 + [SMEM] + [VMEM] * 13, out_specs=[VMEM] * 8,
        scratch_shapes=[pltpu.VMEM((6 * PLANE, LANES), F32), pltpu.VMEM((NE, WIDE, LANES), F32)],
        name="solve",
    )(flat, nbr_src, nbr_idx, orient, *tables, lam, coeff, *operators, *arrived)
    inner, rims = solved[:2]
    returned = exchange(solved[2:])
    out = pl.pallas_call(
        finish_kernel, out_shape=shape((NP * PLANE, LANES), F32), in_specs=[VMEM] * 11, out_specs=VMEM, name="finish",
    )(inner, rims, nbr_src, nbr_idx, orient, *returned)
    return out.reshape(field.shape)


def solution(mesh):
    split_last = P(None, "dev")
    placed = (P(None, None, None, "dev"), P(), P()) + (split_last,) * 7
    return jax.shard_map(
        shards, mesh=mesh, in_specs=placed, out_specs=P(None, None, None, "dev"), check_vma=False
    )
```

profile of v0, /device:TPU:184, one launch (start us, length us, event | category | flops | bytes accessed | tf_op | source)
XLA Modules:
  0.0 67.5 jit_solution(10483326747909646077)
XLA Ops:
  0.0 3.0 %pack.1 = (f32[32,128]{1,0:T(8,128)}, f32[32,128]{1,0:T(8,128)}, f32[32,128]{1,0:T(8,128)}, f32[32,128]{1,0:T(8,128)}, f32[128,128]{1,0:T(8,128)}, /*index=5*/f32[128,128]{1,0:T(8,128)}) custom-call(f32[4096,128]{1,0:T(8,128)} %bitcast.2, s32[2,16]{1,0:T(2,128)} %sx_ref.3, s32[2,16]{1,0:T(2,128)} %sy_ref.3, s32[2,64]{1,0:T(2,128)} %sz_ref.3), custom_call_target="tpu_custom_call" | custom-call | tf_op jit(solution)/shard_map/pack/pallas_call | solution.py:309
  3.0 2.6 %collective-permute-start.4 = (f32[128,128]{1,0:T(8,128)}, f32[128,128]{1,0:T(8,128)S(1)}, u32[]{:S(2)}, u32[]{:S(2)}) collective-permute-start(f32[128,128]{1,0:T(8,128)} %get-tuple-element.35), channel_id=1, source_target_pairs={{16,0},{17,1},{18,2},{19,3},{20,4},{21,5},{22,6},{23,7},{24,8},{25... | collective-permute-start | bytes 196616 | tf_op jit(solution)/shard_map/ppermute | solution.py:301
  5.6 5.3 %collective-permute-start.5 = (f32[128,128]{1,0:T(8,128)}, f32[128,128]{1,0:T(8,128)S(1)}, u32[]{:S(2)}, u32[]{:S(2)}) collective-permute-start(f32[128,128]{1,0:T(8,128)} %get-tuple-element.36), channel_id=1, source_target_pairs={{0,16},{1,17},{2,18},{3,19},{4,20},{5,21},{6,22},{7,23},{8,24},{9,... | collective-permute-start | bytes 196616 | tf_op jit(solution)/shard_map/ppermute | solution.py:301
  11.0 1.9 %collective-permute-start = (f32[32,128]{1,0:T(8,128)}, f32[32,128]{1,0:T(8,128)S(1)}, u32[]{:S(2)}, u32[]{:S(2)}) collective-permute-start(f32[32,128]{1,0:T(8,128)} %get-tuple-element.31), channel_id=1, source_target_pairs={{1,0},{2,1},{3,2},{5,4},{6,5},{7,6},{9,8},{10,9},{11,10},{13,12},{... | collective-permute-start | bytes 49160 | tf_op jit(solution)/shard_map/ppermute | solution.py:301
  12.9 2.4 %collective-permute-start.1 = (f32[32,128]{1,0:T(8,128)}, f32[32,128]{1,0:T(8,128)S(1)}, u32[]{:S(2)}, u32[]{:S(2)}) collective-permute-start(f32[32,128]{1,0:T(8,128)} %get-tuple-element.32), channel_id=1, source_target_pairs={{0,1},{1,2},{2,3},{4,5},{5,6},{6,7},{8,9},{9,10},{10,11},{12,13},{... | collective-permute-start | bytes 49160 | tf_op jit(solution)/shard_map/ppermute | solution.py:301
  15.3 2.5 %collective-permute-start.2 = (f32[32,128]{1,0:T(8,128)}, f32[32,128]{1,0:T(8,128)S(1)}, u32[]{:S(2)}, u32[]{:S(2)}) collective-permute-start(f32[32,128]{1,0:T(8,128)} %get-tuple-element.33), channel_id=1, source_target_pairs={{4,0},{5,1},{6,2},{7,3},{8,4},{9,5},{10,6},{11,7},{12,8},{13,9},{1... | collective-permute-start | bytes 49160 | tf_op jit(solution)/shard_map/ppermute | solution.py:301
  17.8 4.3 %collective-permute-start.3 = (f32[32,128]{1,0:T(8,128)}, f32[32,128]{1,0:T(8,128)S(1)}, u32[]{:S(2)}, u32[]{:S(2)}) collective-permute-start(f32[32,128]{1,0:T(8,128)} %get-tuple-element.34), channel_id=1, source_target_pairs={{0,4},{1,5},{2,6},{3,7},{4,8},{5,9},{6,10},{7,11},{8,12},{9,13},{1... | collective-permute-start | bytes 49160 | tf_op jit(solution)/shard_map/ppermute | solution.py:301
  22.1 4.4 %operators.1 = (bf16[336,768]{1,0:T(8,128)(2,1)}, bf16[336,192]{1,0:T(8,128)(2,1)}, bf16[320,1008]{1,0:T(8,128)(2,1)}, bf16[144,432]{1,0:T(8,128)(2,1)}, bf16[144,432]{1,0:T(8,128)(2,1)}, /*index=5*/f32[336,128]{1,0:T(8,128)}) custom-call(f32[3,18,18]{2,1,0:T(8,128)} %s_ref.1, f32[3,18]{1,0:T(4,128)} %lam_ref.3, f32[3,128]{1,0:T(4,128)} %coeff_ref.3), custom_call_target="tpu_custom_call" | custom-call | tf_op jit(solution)/shard_map/operators/pallas_call | solution.py:313
  26.6 0.5 copy-done.5
  27.1 0.0 copy-done.7
  27.1 0.1 copy-done
  27.2 0.0 copy-done.1
  27.2 10.1 %solve.1 = (f32[4096,128]{1,0:T(8,128)}, f32[1536,128]{1,0:T(8,128)}, f32[32,128]{1,0:T(8,128)}, f32[32,128]{1,0:T(8,128)}, f32[32,128]{1,0:T(8,128)}, /*index=5...) custom-call(f32[4096,128]{1,0:T(8,128)} %bitcast.3, s32[6,128]{1,0:T(8,128)} %src_ref.3, s32[6,128]{1,0:T(8,128)} %idx_ref.3, ...), custom_call_target="tpu_custom_call" | custom-call | tf_op jit(solution)/shard_map/solve/pallas_call | solution.py:321
  37.3 1.9 %collective-permute-start.10 = (f32[128,128]{1,0:T(8,128)}, f32[128,128]{1,0:T(8,128)S(1)}, u32[]{:S(2)}, u32[]{:S(2)}) collective-permute-start(f32[128,128]{1,0:T(8,128)} %get-tuple-element.43), channel_id=1, source_target_pairs={{16,0},{17,1},{18,2},{19,3},{20,4},{21,5},{22,6},{23,7},{24,8},{25... | collective-permute-start | bytes 196616 | tf_op jit(solution)/shard_map/ppermute | solution.py:301
  39.2 6.0 %collective-permute-start.11 = (f32[128,128]{1,0:T(8,128)}, f32[128,128]{1,0:T(8,128)S(1)}, u32[]{:S(2)}, u32[]{:S(2)}) collective-permute-start(f32[128,128]{1,0:T(8,128)} %get-tuple-element.44), channel_id=1, source_target_pairs={{0,16},{1,17},{2,18},{3,19},{4,20},{5,21},{6,22},{7,23},{8,24},{9,... | collective-permute-start | bytes 196616 | tf_op jit(solution)/shard_map/ppermute | solution.py:301
  45.2 2.1 %collective-permute-start.6 = (f32[32,128]{1,0:T(8,128)}, f32[32,128]{1,0:T(8,128)S(1)}, u32[]{:S(2)}, u32[]{:S(2)}) collective-permute-start(f32[32,128]{1,0:T(8,128)} %get-tuple-element.39), channel_id=1, source_target_pairs={{1,0},{2,1},{3,2},{5,4},{6,5},{7,6},{9,8},{10,9},{11,10},{13,12},{... | collective-permute-start | bytes 49160 | tf_op jit(solution)/shard_map/ppermute | solution.py:301
  47.3 2.3 %collective-permute-start.7 = (f32[32,128]{1,0:T(8,128)}, f32[32,128]{1,0:T(8,128)S(1)}, u32[]{:S(2)}, u32[]{:S(2)}) collective-permute-start(f32[32,128]{1,0:T(8,128)} %get-tuple-element.40), channel_id=1, source_target_pairs={{0,1},{1,2},{2,3},{4,5},{5,6},{6,7},{8,9},{9,10},{10,11},{12,13},{... | collective-permute-start | bytes 49160 | tf_op jit(solution)/shard_map/ppermute | solution.py:301
  49.6 3.7 %collective-permute-start.8 = (f32[32,128]{1,0:T(8,128)}, f32[32,128]{1,0:T(8,128)S(1)}, u32[]{:S(2)}, u32[]{:S(2)}) collective-permute-start(f32[32,128]{1,0:T(8,128)} %get-tuple-element.41), channel_id=1, source_target_pairs={{4,0},{5,1},{6,2},{7,3},{8,4},{9,5},{10,6},{11,7},{12,8},{13,9},{1... | collective-permute-start | bytes 49160 | tf_op jit(solution)/shard_map/ppermute | solution.py:301
  53.3 3.0 %collective-permute-start.9 = (f32[32,128]{1,0:T(8,128)}, f32[32,128]{1,0:T(8,128)S(1)}, u32[]{:S(2)}, u32[]{:S(2)}) collective-permute-start(f32[32,128]{1,0:T(8,128)} %get-tuple-element.42), channel_id=1, source_target_pairs={{0,4},{1,5},{2,6},{3,7},{4,8},{5,9},{6,10},{7,11},{8,12},{9,13},{1... | collective-permute-start | bytes 49160 | tf_op jit(solution)/shard_map/ppermute | solution.py:301
  56.4 5.1 %collective-permute-done.9.m3 = f32[32,128]{1,0:T(8,128)S(1)} collective-permute-done((f32[32,128]{1,0:T(8,128)}, f32[32,128]{1,0:T(8,128)S(1)}, u32[]{:S(2)}, u32[]{:S(2)}) %collective-permute-start.9) | collective-permute-done | bytes 16416 | tf_op jit(solution)/shard_map/ppermute | solution.py:301
  61.6 0.5 copy-done.11
  62.1 0.0 copy-done.2
  62.1 0.0 copy-done.3
  62.2 5.4 %finish.1 = f32[4096,128]{1,0:T(8,128)} custom-call(f32[4096,128]{1,0:T(8,128)} %get-tuple-element.37.inner_ref, f32[1536,128]{1,0:T(8,128)} %get-tuple-element.38.rim_ref, s32[6,128]{1,0:T(8,128)} %src_ref.3, s32[6,128]{1,0:T(8,128)} %idx_ref.3, s32[6,128]{1,0:T(8,128)} %code_ref.3, f32[32,128]{1,0:T(8,128)} %copy-done.8, f32[32,128]{1,0:T(8,128)} %copy-done.9, ...), custom_call_target="tpu_custom_call" | custom-call | tf_op jit(solution)/shard_map/finish/pallas_call | solution.py:330
  (28 shorter events, 0.1 us)
Async XLA Ops:
  3.0 23.5 %collective-permute-start.4 = (f32[128,128]{1,0:T(8,128)}, f32[128,128]{1,0:T(8,128)S(1)}, u32[]{:S(2)}, u32[]{:S(2)}) collective-permute-start(f32[128,128]{1,0:T(8,128)} %get-tuple-element.35), channel_id=1, source_target_pairs={{16,0},{17,1},{18,2},{19,3},{20,4},{21,5},{22,6},{23,7},{24,8},{25... | collective-permute-start | bytes 196616 | tf_op jit(solution)/shard_map/ppermute | solution.py:301
  5.6 20.9 %collective-permute-start.5 = (f32[128,128]{1,0:T(8,128)}, f32[128,128]{1,0:T(8,128)S(1)}, u32[]{:S(2)}, u32[]{:S(2)}) collective-permute-start(f32[128,128]{1,0:T(8,128)} %get-tuple-element.36), channel_id=1, source_target_pairs={{0,16},{1,17},{2,18},{3,19},{4,20},{5,21},{6,22},{7,23},{8,24},{9,... | collective-permute-start | bytes 196616 | tf_op jit(solution)/shard_map/ppermute | solution.py:301
  11.0 6.8 %collective-permute-start = (f32[32,128]{1,0:T(8,128)}, f32[32,128]{1,0:T(8,128)S(1)}, u32[]{:S(2)}, u32[]{:S(2)}) collective-permute-start(f32[32,128]{1,0:T(8,128)} %get-tuple-element.31), channel_id=1, source_target_pairs={{1,0},{2,1},{3,2},{5,4},{6,5},{7,6},{9,8},{10,9},{11,10},{13,12},{... | collective-permute-start | bytes 49160 | tf_op jit(solution)/shard_map/ppermute | solution.py:301
  12.9 13.6 %collective-permute-start.1 = (f32[32,128]{1,0:T(8,128)}, f32[32,128]{1,0:T(8,128)S(1)}, u32[]{:S(2)}, u32[]{:S(2)}) collective-permute-start(f32[32,128]{1,0:T(8,128)} %get-tuple-element.32), channel_id=1, source_target_pairs={{0,1},{1,2},{2,3},{4,5},{5,6},{6,7},{8,9},{9,10},{10,11},{12,13},{... | collective-permute-start | bytes 49160 | tf_op jit(solution)/shard_map/ppermute | solution.py:301
  15.3 11.2 %collective-permute-start.2 = (f32[32,128]{1,0:T(8,128)}, f32[32,128]{1,0:T(8,128)S(1)}, u32[]{:S(2)}, u32[]{:S(2)}) collective-permute-start(f32[32,128]{1,0:T(8,128)} %get-tuple-element.33), channel_id=1, source_target_pairs={{4,0},{5,1},{6,2},{7,3},{8,4},{9,5},{10,6},{11,7},{12,8},{13,9},{1... | collective-permute-start | bytes 49160 | tf_op jit(solution)/shard_map/ppermute | solution.py:301
  17.8 8.8 %copy-start.4 = (f32[32,128]{1,0:T(8,128)}, f32[32,128]{1,0:T(8,128)S(1)}, u32[]{:S(2)}) copy-start(f32[32,128]{1,0:T(8,128)S(1)} %collective-permute-done.m0) | copy-start | bytes 49156
  17.8 8.7 %collective-permute-start.3 = (f32[32,128]{1,0:T(8,128)}, f32[32,128]{1,0:T(8,128)S(1)}, u32[]{:S(2)}, u32[]{:S(2)}) collective-permute-start(f32[32,128]{1,0:T(8,128)} %get-tuple-element.34), channel_id=1, source_target_pairs={{0,4},{1,5},{2,6},{3,7},{4,8},{5,9},{6,10},{7,11},{8,12},{9,13},{1... | collective-permute-start | bytes 49160 | tf_op jit(solution)/shard_map/ppermute | solution.py:301
  26.5 0.6 copy-start.5
  26.5 0.6 copy-start.6
  26.5 0.6 copy-start.7
  26.5 0.6 copy-start
  26.5 0.6 copy-start.1
  37.3 24.3 %collective-permute-start.10 = (f32[128,128]{1,0:T(8,128)}, f32[128,128]{1,0:T(8,128)S(1)}, u32[]{:S(2)}, u32[]{:S(2)}) collective-permute-start(f32[128,128]{1,0:T(8,128)} %get-tuple-element.43), channel_id=1, source_target_pairs={{16,0},{17,1},{18,2},{19,3},{20,4},{21,5},{22,6},{23,7},{24,8},{25... | collective-permute-start | bytes 196616 | tf_op jit(solution)/shard_map/ppermute | solution.py:301
  39.2 22.3 %collective-permute-start.11 = (f32[128,128]{1,0:T(8,128)}, f32[128,128]{1,0:T(8,128)S(1)}, u32[]{:S(2)}, u32[]{:S(2)}) collective-permute-start(f32[128,128]{1,0:T(8,128)} %get-tuple-element.44), channel_id=1, source_target_pairs={{0,16},{1,17},{2,18},{3,19},{4,20},{5,21},{6,22},{7,23},{8,24},{9,... | collective-permute-start | bytes 196616 | tf_op jit(solution)/shard_map/ppermute | solution.py:301
  45.2 8.1 %collective-permute-start.6 = (f32[32,128]{1,0:T(8,128)}, f32[32,128]{1,0:T(8,128)S(1)}, u32[]{:S(2)}, u32[]{:S(2)}) collective-permute-start(f32[32,128]{1,0:T(8,128)} %get-tuple-element.39), channel_id=1, source_target_pairs={{1,0},{2,1},{3,2},{5,4},{6,5},{7,6},{9,8},{10,9},{11,10},{13,12},{... | collective-permute-start | bytes 49160 | tf_op jit(solution)/shard_map/ppermute | solution.py:301
  47.3 9.0 %collective-permute-start.7 = (f32[32,128]{1,0:T(8,128)}, f32[32,128]{1,0:T(8,128)S(1)}, u32[]{:S(2)}, u32[]{:S(2)}) collective-permute-start(f32[32,128]{1,0:T(8,128)} %get-tuple-element.40), channel_id=1, source_target_pairs={{0,1},{1,2},{2,3},{4,5},{5,6},{6,7},{8,9},{9,10},{10,11},{12,13},{... | collective-permute-start | bytes 49160 | tf_op jit(solution)/shard_map/ppermute | solution.py:301
  49.6 6.8 %collective-permute-start.8 = (f32[32,128]{1,0:T(8,128)}, f32[32,128]{1,0:T(8,128)S(1)}, u32[]{:S(2)}, u32[]{:S(2)}) collective-permute-start(f32[32,128]{1,0:T(8,128)} %get-tuple-element.41), channel_id=1, source_target_pairs={{4,0},{5,1},{6,2},{7,3},{8,4},{9,5},{10,6},{11,7},{12,8},{13,9},{1... | collective-permute-start | bytes 49160 | tf_op jit(solution)/shard_map/ppermute | solution.py:301
  53.3 8.2 %copy-start.8 = (f32[32,128]{1,0:T(8,128)}, f32[32,128]{1,0:T(8,128)S(1)}, u32[]{:S(2)}) copy-start(f32[32,128]{1,0:T(8,128)S(1)} %collective-permute-done.6.m0) | copy-start | bytes 49156
  53.3 8.2 %collective-permute-start.9 = (f32[32,128]{1,0:T(8,128)}, f32[32,128]{1,0:T(8,128)S(1)}, u32[]{:S(2)}, u32[]{:S(2)}) collective-permute-start(f32[32,128]{1,0:T(8,128)} %get-tuple-element.42), channel_id=1, source_target_pairs={{0,4},{1,5},{2,6},{3,7},{4,8},{5,9},{6,10},{7,11},{8,12},{9,13},{1... | collective-permute-start | bytes 49160 | tf_op jit(solution)/shard_map/ppermute | solution.py:301
  56.3 5.2 %copy-start.9 = (f32[32,128]{1,0:T(8,128)}, f32[32,128]{1,0:T(8,128)S(1)}, u32[]{:S(2)}) copy-start(f32[32,128]{1,0:T(8,128)S(1)} %collective-permute-done.7.m1) | copy-start | bytes 49156
  56.4 5.2 %copy-start.10 = (f32[32,128]{1,0:T(8,128)}, f32[32,128]{1,0:T(8,128)S(1)}, u32[]{:S(2)}) copy-start(f32[32,128]{1,0:T(8,128)S(1)} %collective-permute-done.8.m2) | copy-start | bytes 49156
  61.5 0.6 copy-start.11
  61.5 0.6 copy-start.2
  61.5 0.7 copy-start.3
where the time goes:
time: 68.1 us; the launch traced here: 67.5 us
  starting transfers between devices  38 us (56%)
  Pallas kernels  22.8 us (33%)
  waiting for transfers between devices  5.16 us (8%)
  local copies, waits for them, and re-layouts  1.27 us (2%)
    ppermute x12, starting transfers between devices, exchange(): arrived.append(lax.ppermute(messages[direction], 'dev', pairs))  38 us
    pallas_call x1, Pallas kernels, shards(): pl.pallas_call(solve_kernel, out_shape=[shape((NP * PLANE, LANES), F32),...  10.1 us
    pallas_call x1, Pallas kernels, shards(): pl.pallas_call(finish_kernel, out_shape=shape((NP * PLANE, LANES), F32),...  5.35 us
    ppermute x12, waiting for transfers between devices, exchange(): arrived.append(lax.ppermute(messages[direction], 'dev', pairs))  5.16 us
    pallas_call x1, Pallas kernels, shards(): pl.pallas_call(operators_kernel, out_shape=[shape((WIDE, 3 * PLANE), BF16...  4.41 us
    pallas_call x1, Pallas kernels, shards(): pl.pallas_call(pack_kernel, out_shape=message_shapes(tables), in_specs=[V...  3 us
  transfers between devices with their start and end apart: 12, of which 1 were waited for; matrix products, arithmetic and copies ran while one was open for 0% of the time, Pallas kernels for 7%

commit v1 on v0

--- a/solution.py
+++ b/solution.py
@@ -1,5 +1,3 @@
-import functools
-
 import jax
 import jax.numpy as jnp
 from jax import lax
@@ -7,9 +5,10 @@
 from jax.experimental.pallas import tpu as pltpu
 from jax.sharding import PartitionSpec as P
 
+
 DEV_X = 4
 DEV_Y = 4
-OFFSETS = (-1, 1, -DEV_X, DEV_X, -DEV_X * DEV_Y, DEV_X * DEV_Y)
+ORDER = (5, 0, 3, 1, 4, 2)
 NP = 16
 NE = 18
 PLANE = NP * NP
@@ -22,16 +21,23 @@
 BF16 = jnp.bfloat16
 
 
-def neighbour_pairs(direction, size):
-    axis = direction // 2
-    step = 1 if direction % 2 else -1
+def swap_pairs(axis, turn, size):
     layout = (DEV_X, DEV_Y, size // (DEV_X * DEV_Y))
+    stride = (1, DEV_X, DEV_X * DEV_Y)[axis]
     pairs = []
     for i in range(size):
-        place = (i % DEV_X, i // DEV_X % DEV_Y, i // (DEV_X * DEV_Y))
-        if 0 <= place[axis] + step < layout[axis]:
-            pairs.append((i, i + OFFSETS[direction]))
+        place = i // stride % layout[axis]
+        other = place + 1 if place % 2 == turn else place - 1
+        if 0 <= other < layout[axis]:
+            pairs.append((i, i + (other - place) * stride))
+        else:
+            pairs.append((i, i ^ (DEV_X - 1 if axis == 0 else 1)))
     return pairs
+
+
+def odd_place(axis):
+    stride = (1, DEV_X, DEV_X * DEV_Y)[axis]
+    return (lax.axis_index("dev") // stride) % 2 == 1
 
 
 def lane_take(values, index):
@@ -42,34 +48,35 @@
     return lax.broadcasted_iota(jnp.int32, shape, 1)
 
 
-def pack_axis(axis, plane, table, low_ref, high_ref):
+def pack_axis(axis, plane, table, odd, first_ref, second_ref):
     count = table.shape[1]
     blocks = LANES // count
     rows = PLANE // blocks
-    low, high = table[0:1], table[1:2]
-    forward = jnp.concatenate([low, high] * (blocks // 2), axis=1)
-    backward = jnp.concatenate([high, low] * (blocks // 2), axis=1)
+    first = jnp.where(odd, table[0:1], table[1:2])
+    second = jnp.where(odd, table[1:2], table[0:1])
+    forward = jnp.concatenate([first, second] * (blocks // 2), axis=1)
+    backward = jnp.concatenate([second, first] * (blocks // 2), axis=1)
     patterns = []
     for ids in (forward, backward):
         ids = jnp.broadcast_to(ids, (8, LANES))
         patterns.append((ids & (LANES - 1), (ids // LANES) == 2 * axis + 1))
     lane_block = lanes((8, LANES)) // count
     for row in range(0, rows, 8):
-        low_value = jnp.zeros((8, LANES), F32)
-        high_value = jnp.zeros((8, LANES), F32)
+        first_value = jnp.zeros((8, LANES), F32)
+        second_value = jnp.zeros((8, LANES), F32)
         for block in range(blocks):
             slot, is_high = patterns[block % 2]
             start = block * rows + row
             got = jnp.where(is_high, lane_take(plane(1, start), slot), lane_take(plane(0, start), slot))
-            low_value = jnp.where(lane_block == block, got, low_value)
-            high_value = jnp.where(lane_block == block ^ 1, got, high_value)
-        low_ref[row : row + 8] = low_value
-        high_ref[row : row + 8] = high_value
-
-
-def unpack_face(face, plane, low_ref, high_ref, source, index, code, put):
+            first_value = jnp.where(lane_block == block, got, first_value)
+            second_value = jnp.where(lane_block == block ^ 1, got, second_value)
+        first_ref[row : row + 8] = first_value
+        second_ref[row : row + 8] = second_value
+
+
+def unpack_face(face, plane, odd, first_ref, second_ref, source, index, code, put):
     axis = face // 2
-    rows = low_ref.shape[0]
+    rows = first_ref.shape[0]
     blocks = PLANE // rows
     count = LANES // blocks
     full = lambda row: jnp.broadcast_to(row, (8, LANES))
@@ -77,8 +84,8 @@
     slot = index & (LANES - 1)
     local_high = (source == 1) & ((index // LANES) == 2 * axis + 1)
     local = source == 1
-    from_low = source == 2 + 2 * axis
-    from_high = source == 3 + 2 * axis
+    from_first = source == jnp.where(odd, 3 + 2 * axis, 2 + 2 * axis)
+    from_second = source == jnp.where(odd, 2 + 2 * axis, 3 + 2 * axis)
     position = index & (count - 1)
     flip_first = (code & 1) == 1
     flip_second = (code & 2) == 2
@@ -87,9 +94,9 @@
     def fetch(start):
         block, row = start // rows, start % rows
         here = jnp.where(local_high, lane_take(plane(1, start), slot), lane_take(plane(0, start), slot))
-        low = lane_take(low_ref[row : row + 8], position + block * count)
-        high = lane_take(high_ref[row : row + 8], position + (block ^ 1) * count)
-        away = jnp.where(from_low, low, jnp.where(from_high, high, 0.0))
+        one = lane_take(first_ref[row : row + 8], position + block * count)
+        two = lane_take(second_ref[row : row + 8], position + (block ^ 1) * count)
+        away = jnp.where(from_first, one, jnp.where(from_second, two, 0.0))
         return jnp.where(local, here, away)
 
     def turn(value):
@@ -126,7 +133,7 @@
 
 def pack_kernel(field_ref, sx_ref, sy_ref, sz_ref, *out_refs):
     for axis, table_ref in enumerate((sx_ref, sy_ref, sz_ref)):
-        pack_axis(axis, field_plane(field_ref, axis), table_ref[...], out_refs[2 * axis], out_refs[2 * axis + 1])
+        pack_axis(axis, field_plane(field_ref, axis), table_ref[...], odd_place(axis), out_refs[2 * axis], out_refs[2 * axis + 1])
 
 
 def split(value):
@@ -209,7 +216,7 @@
                 ghost_ref[pl.ds(face * PLANE + line * NP + 8 * h, 8)] = pieces[h]
 
         unpack_face(
-            face, field_plane(field_ref, axis), messages[2 * axis], messages[2 * axis + 1],
+            face, field_plane(field_ref, axis), odd_place(axis), messages[2 * axis], messages[2 * axis + 1],
             src_ref[face : face + 1], idx_ref[face : face + 1], code_ref[face : face + 1], put,
         )
 
@@ -256,7 +263,7 @@
                 start = PLANE + (f - 2) * NP
                 rim_ref[f * PLANE + i * NP : f * PLANE + (i + 1) * NP] = part[start : start + NP]
     for axis, table_ref in enumerate((sx_ref, sy_ref, sz_ref)):
-        pack_axis(axis, rim_plane(rim_ref, axis), table_ref[...], outs[2 * axis], outs[2 * axis + 1])
+        pack_axis(axis, rim_plane(rim_ref, axis), table_ref[...], odd_place(axis), outs[2 * axis], outs[2 * axis + 1])
 
 
 def finish_kernel(inner_ref, rim_ref, src_ref, idx_ref, code_ref, m0, m1, m2, m3, m4, m5, out_ref):
@@ -277,13 +284,17 @@
                 out_ref[place] = out_ref[place] + pieces[h]
 
         unpack_face(
-            face, rim_plane(rim_ref, axis), messages[2 * axis], messages[2 * axis + 1],
+            face, rim_plane(rim_ref, axis), odd_place(axis), messages[2 * axis], messages[2 * axis + 1],
             src_ref[face : face + 1], idx_ref[face : face + 1], code_ref[face : face + 1], put,
         )
 
 
 VMEM = pl.BlockSpec(memory_space=pltpu.VMEM)
 SMEM = pl.BlockSpec(memory_space=pltpu.SMEM)
+
+
+def grant(mebibytes):
+    return pltpu.CompilerParams(vmem_limit_bytes=mebibytes << 20)
 
 
 def message_shapes(tables):
@@ -295,10 +306,10 @@
 
 
 def exchange(messages):
-    arrived = []
-    for direction in range(6):
-        pairs = neighbour_pairs(direction, lax.axis_size("dev"))
-        arrived.append(lax.ppermute(messages[direction], "dev", pairs))
+    arrived = [None] * 6
+    for number in ORDER:
+        pairs = swap_pairs(number // 2, number % 2, lax.axis_size("dev"))
+        arrived[number] = lax.ppermute(messages[number], "dev", pairs)
     return arrived
 
 
@@ -308,6 +319,7 @@
     shape = jax.ShapeDtypeStruct
     outgoing = pl.pallas_call(
         pack_kernel, out_shape=message_shapes(tables), in_specs=[VMEM] * 4, out_specs=[VMEM] * 6, name="pack",
+        compiler_params=grant(8),
     )(flat, *tables)
     arrived = exchange(outgoing)
     operators = pl.pallas_call(
@@ -317,18 +329,20 @@
             shape((DEEP, 3 * DEEP), BF16), shape((DEEP, 3 * DEEP), BF16), shape((WIDE, LANES), F32),
         ],
         in_specs=[VMEM] * 3, out_specs=[VMEM] * 6, name="operators",
+        compiler_params=grant(16),
     )(s_mats, lam, coeff)
     solved = pl.pallas_call(
         solve_kernel,
         out_shape=[shape((NP * PLANE, LANES), F32), shape((6 * PLANE, LANES), F32)] + message_shapes(tables),
         in_specs=[VMEM] * 7 + [SMEM] + [VMEM] * 13, out_specs=[VMEM] * 8,
         scratch_shapes=[pltpu.VMEM((6 * PLANE, LANES), F32), pltpu.VMEM((NE, WIDE, LANES), F32)],
-        name="solve",
+        name="solve", compiler_params=grant(24),
     )(flat, nbr_src, nbr_idx, orient, *tables, lam, coeff, *operators, *arrived)
     inner, rims = solved[:2]
     returned = exchange(solved[2:])
     out = pl.pallas_call(
         finish_kernel, out_shape=shape((NP * PLANE, LANES), F32), in_specs=[VMEM] * 11, out_specs=VMEM, name="finish",
+        compiler_params=grant(12),
     )(inner, rims, nbr_src, nbr_idx, orient, *returned)
     return out.reshape(field.shape)
 
@@ -336,6 +350,4 @@
 def solution(mesh):
     split_last = P(None, "dev")
     placed = (P(None, None, None, "dev"), P(), P()) + (split_last,) * 7
-    return jax.shard_map(
-        shards, mesh=mesh, in_specs=placed, out_specs=P(None, None, None, "dev"), check_vma=False
-    )
+    return jax.shard_map(shards, mesh=mesh, in_specs=placed, out_specs=P(None, None, None, "dev"), check_vma=False)

time: 68.1 us -> 42 us (0.62)
  the two profiles are of different devices: /device:TPU:184 before, /device:TPU:68 now
where the time goes in v1:
time: 42 us; the launch traced here: 41.7 us
  starting transfers between devices  15.9 us (38%)
  Pallas kernels  14.1 us (34%)
  local copies, waits for them, and re-layouts  7.14 us (17%)
  waiting for transfers between devices  4.47 us (11%)
    ppermute x12, starting transfers between devices, exchange(): arrived[number] = lax.ppermute(messages[number], 'dev', pairs)  15.9 us
    unnamed x30, local copies, waits for them, and re-layouts  7.14 us
    pallas_call x1, Pallas kernels, shards(): pl.pallas_call(solve_kernel, out_shape=[shape((NP * PLANE, LANES), F32),...  7.05 us
    ppermute x12, waiting for transfers between devices, exchange(): arrived[number] = lax.ppermute(messages[number], 'dev', pairs)  4.47 us
    pallas_call x1, Pallas kernels, shards(): pl.pallas_call(finish_kernel, out_shape=shape((NP * PLANE, LANES), F32),...  3.45 us
    pallas_call x1, Pallas kernels, shards(): pl.pallas_call(operators_kernel, out_shape=[shape((WIDE, 3 * PLANE), BF16...  2.86 us
  transfers between devices with their start and end apart: 12, of which 4 were waited for; matrix products, arithmetic and copies ran while one was open for 0% of the time, Pallas kernels for 7%

profile of v1, /device:TPU:68, one launch (start us, length us, event | category | flops | bytes accessed | tf_op | source)
XLA Modules:
  0.0 41.7 jit_solution(15962335511280823334)
XLA Ops:
  0.0 1.6 %copy-done = f32[16,16,16,128]{3,2,1,0:T(8,128)S(1)} copy-done((f32[16,16,16,128]{3,2,1,0:T(8,128)S(1)}, f32[16,16,16,128]{3,2,1,0:T(8,128)}, u32[]{:S(2)}) %copy-start) | copy-done | bytes 2097176
  1.6 0.7 %copy-done.9 = s32[2,16]{1,0:T(2,128)S(1)} copy-done((s32[2,16]{1,0:T(2,128)S(1)}, s32[2,16]{1,0:T(2,128)}, u32[]{:S(2)}) %copy-start.9) | copy-done | bytes 152
  2.3 0.7 %copy-done.11 = s32[2,16]{1,0:T(2,128)S(1)} copy-done((s32[2,16]{1,0:T(2,128)S(1)}, s32[2,16]{1,0:T(2,128)}, u32[]{:S(2)}) %copy-start.11) | copy-done | bytes 152
  3.0 0.7 %copy-done.13 = s32[2,64]{1,0:T(2,128)S(1)} copy-done((s32[2,64]{1,0:T(2,128)S(1)}, s32[2,64]{1,0:T(2,128)}, u32[]{:S(2)}) %copy-start.13) | copy-done | bytes 536
  3.7 0.7 %pack.1 = (f32[32,128]{1,0:T(8,128)S(1)}, f32[32,128]{1,0:T(8,128)S(1)}, f32[32,128]{1,0:T(8,128)S(1)}, f32[32,128]{1,0:T(8,128)S(1)}, f32[128,128]{1,0:T(8,128)S(1)}, /*index=5*/f32[128,128]{1,0:T(8,128)S(1)}) custom-call(f32[4096,128]{1,0:T(8,128)S(1)} %bitcast.2, s32[2,16]{1,0:T(2,128)S(1)} %copy-done.9, s32[2,16]{1,0:T(2,128)S(1)} %copy-done.11, ...), custom_call_target="tpu_custom_call" | custom-call | tf_op jit(solution)/shard_map/pack/pallas_call | solution.py:320
  4.4 1.7 %collective-permute-start.4 = (f32[128,128]{1,0:T(8,128)S(1)}, f32[128,128]{1,0:T(8,128)S(1)}, u32[]{:S(2)}, u32[]{:S(2)}) collective-permute-start(f32[128,128]{1,0:T(8,128)S(1)} %get-tuple-element.35), channel_id=1, source_target_pairs={{0,16},{1,17},{2,18},{3,19},{4,20},{5,21},{6,22},{7,23},{8,24},{9,... | collective-permute-start | bytes 196616 | tf_op jit(solution)/shard_map/ppermute | solution.py:312
  6.1 2.2 %collective-permute-start.5 = (f32[128,128]{1,0:T(8,128)S(1)}, f32[128,128]{1,0:T(8,128)S(1)}, u32[]{:S(2)}, u32[]{:S(2)}) collective-permute-start(f32[128,128]{1,0:T(8,128)S(1)} %get-tuple-element.36), channel_id=1, source_target_pairs={{0,1},{1,0},{2,3},{3,2},{4,5},{5,4},{6,7},{7,6},{8,9},{9,8},{10,11... | collective-permute-start | bytes 196616 | tf_op jit(solution)/shard_map/ppermute | solution.py:312
  8.2 2.0 %collective-permute-start.1 = (f32[32,128]{1,0:T(8,128)S(1)}, f32[32,128]{1,0:T(8,128)S(1)}, u32[]{:S(2)}, u32[]{:S(2)}) collective-permute-start(f32[32,128]{1,0:T(8,128)S(1)} %get-tuple-element.32), channel_id=1, source_target_pairs={{0,3},{1,2},{2,1},{3,0},{4,7},{5,6},{6,5},{7,4},{8,11},{9,10},{10,... | collective-permute-start | bytes 49160 | tf_op jit(solution)/shard_map/ppermute | solution.py:312
  10.3 5.1 %collective-permute-start.3 = (f32[32,128]{1,0:T(8,128)S(1)}, f32[32,128]{1,0:T(8,128)S(1)}, u32[]{:S(2)}, u32[]{:S(2)}) collective-permute-start(f32[32,128]{1,0:T(8,128)S(1)} %get-tuple-element.34), channel_id=1, source_target_pairs={{0,1},{1,0},{2,3},{3,2},{4,8},{5,9},{6,10},{7,11},{8,4},{9,5},{10,... | collective-permute-start | bytes 49160 | tf_op jit(solution)/shard_map/ppermute | solution.py:312
  15.3 0.8 %copy-done.2 = f32[3,18,18]{2,1,0:T(8,128)S(1)} copy-done((f32[3,18,18]{2,1,0:T(8,128)S(1)}, f32[3,18,18]{2,1,0:T(8,128)}, u32[]{:S(2)}) %copy-start.2) | copy-done | bytes 3912
  16.1 0.7 %copy-done.7 = f32[3,128]{1,0:T(4,128)S(1)} copy-done((f32[3,128]{1,0:T(4,128)S(1)}, f32[3,128]{1,0:T(4,128)}, u32[]{:S(2)}) %copy-start.7) | copy-done | bytes 1560
  16.8 2.9 %operators.1 = (bf16[336,768]{1,0:T(8,128)(2,1)S(1)}, bf16[336,192]{1,0:T(8,128)(2,1)S(1)}, bf16[320,1008]{1,0:T(8,128)(2,1)S(1)}, bf16[144,432]{1,0:T(8,128)(2,...) custom-call(f32[3,18,18]{2,1,0:T(8,128)S(1)} %copy-done.2, f32[3,18]{1,0:T(4,128)S(1)} %copy-done.6, ...), custom_call_target="tpu_custom_call" | custom-call | tf_op jit(solution)/shard_map/operators/pallas_call | solution.py:325
  19.7 0.7 %copy-done.8 = f32[3,128]{1,0:T(4,128)S(1)} copy-done((f32[3,128]{1,0:T(4,128)S(1)}, f32[3,128]{1,0:T(4,128)}, u32[]{:S(2)}) %copy-start.8) | copy-done | bytes 1560
  20.4 0.7 %copy-done.12 = s32[2,16]{1,0:T(2,128)S(1)} copy-done((s32[2,16]{1,0:T(2,128)S(1)}, s32[2,16]{1,0:T(2,128)}, u32[]{:S(2)}) %copy-start.12) | copy-done | bytes 152
  21.1 0.7 %copy-done.14 = s32[2,64]{1,0:T(2,128)S(1)} copy-done((s32[2,64]{1,0:T(2,128)S(1)}, s32[2,64]{1,0:T(2,128)}, u32[]{:S(2)}) %copy-start.14) | copy-done | bytes 536
  21.8 7.1 %solve.1 = (f32[4096,128]{1,0:T(8,128)S(1)}, f32[1536,128]{1,0:T(8,128)S(1)}, f32[32,128]{1,0:T(8,128)S(1)}, f32[32,128]{1,0:T(8,128)S(1)}, f32[32,128]{1,0:T(8,...) custom-call(f32[4096,128]{1,0:T(8,128)S(1)} %bitcast.3, s32[6,128]{1,0:T(8,128)S(1)} %copy-done.3, ...), custom_call_target="tpu_custom_call" | custom-call | tf_op jit(solution)/shard_map/solve/pallas_call | solution.py:334
  28.8 1.0 %collective-permute-start.10 = (f32[128,128]{1,0:T(8,128)S(1)}, f32[128,128]{1,0:T(8,128)S(1)}, u32[]{:S(2)}, u32[]{:S(2)}) collective-permute-start(f32[128,128]{1,0:T(8,128)S(1)} %get-tuple-element.43), channel_id=1, source_target_pairs={{0,16},{1,17},{2,18},{3,19},{4,20},{5,21},{6,22},{7,23},{8,24},{9,... | collective-permute-start | bytes 196616 | tf_op jit(solution)/shard_map/ppermute | solution.py:312
  29.8 1.4 %collective-permute-start.11 = (f32[128,128]{1,0:T(8,128)S(1)}, f32[128,128]{1,0:T(8,128)S(1)}, u32[]{:S(2)}, u32[]{:S(2)}) collective-permute-start(f32[128,128]{1,0:T(8,128)S(1)} %get-tuple-element.44), channel_id=1, source_target_pairs={{0,1},{1,0},{2,3},{3,2},{4,5},{5,4},{6,7},{7,6},{8,9},{9,8},{10,11... | collective-permute-start | bytes 196616 | tf_op jit(solution)/shard_map/ppermute | solution.py:312
  31.2 1.1 %collective-permute-start.7 = (f32[32,128]{1,0:T(8,128)S(1)}, f32[32,128]{1,0:T(8,128)S(1)}, u32[]{:S(2)}, u32[]{:S(2)}) collective-permute-start(f32[32,128]{1,0:T(8,128)S(1)} %get-tuple-element.40), channel_id=1, source_target_pairs={{0,3},{1,2},{2,1},{3,0},{4,7},{5,6},{6,5},{7,4},{8,11},{9,10},{10,... | collective-permute-start | bytes 49160 | tf_op jit(solution)/shard_map/ppermute | solution.py:312
  32.4 1.5 %collective-permute-start.9 = (f32[32,128]{1,0:T(8,128)S(1)}, f32[32,128]{1,0:T(8,128)S(1)}, u32[]{:S(2)}, u32[]{:S(2)}) collective-permute-start(f32[32,128]{1,0:T(8,128)S(1)} %get-tuple-element.42), channel_id=1, source_target_pairs={{0,1},{1,0},{2,3},{3,2},{4,8},{5,9},{6,10},{7,11},{8,4},{9,5},{10,... | collective-permute-start | bytes 49160 | tf_op jit(solution)/shard_map/ppermute | solution.py:312
  33.9 0.5 %collective-permute-done.7.m1 = f32[32,128]{1,0:T(8,128)S(1)} collective-permute-done((f32[32,128]{1,0:T(8,128)S(1)}, f32[32,128]{1,0:T(8,128)S(1)}, u32[]{:S(2)}, u32[]{:S(2)}) %collective-permute-start.7) | collective-permute-done | bytes 16416 | tf_op jit(solution)/shard_map/ppermute | solution.py:312
  34.4 2.6 %collective-permute-done.8.m2 = f32[32,128]{1,0:T(8,128)S(1)} collective-permute-done((f32[32,128]{1,0:T(8,128)S(1)}, f32[32,128]{1,0:T(8,128)S(1)}, u32[]{:S(2)}, u32[]{:S(2)}) %collective-permute-start.8) | collective-permute-done | bytes 16416 | tf_op jit(solution)/shard_map/ppermute | solution.py:312
  37.0 1.3 %collective-permute-done.9.m3 = f32[32,128]{1,0:T(8,128)S(1)} collective-permute-done((f32[32,128]{1,0:T(8,128)S(1)}, f32[32,128]{1,0:T(8,128)S(1)}, u32[]{:S(2)}, u32[]{:S(2)}) %collective-permute-start.9) | collective-permute-done | bytes 16416 | tf_op jit(solution)/shard_map/ppermute | solution.py:312
  38.3 3.4 %finish.1 = f32[4096,128]{1,0:T(8,128)} custom-call(f32[4096,128]{1,0:T(8,128)S(1)} %get-tuple-element.37.inner_ref, f32[1536,128]{1,0:T(8,128)S(1)} %get-tuple-element.38.rim_ref, s32[6,128]{1,0:T(8,128)S(1)} %copy-done.3, s32[6,128]{1,0:T(8,128)S(1)} %copy-done.4, s32[6,128]{1,0:T(8,128)S(1)} %copy-done.5, f32[32,128]{1,0:T(8,128)S(1)} %collective-permute-done.6.m0, ...), custom_call_target="tpu_custom_call" | custom-call | tf_op jit(solution)/shard_map/finish/pallas_call | solution.py:343
  (34 shorter events, 0.1 us)
Async XLA Ops:
  0.0 19.7 %copy-start.10 = (s32[2,16]{1,0:T(2,128)S(1)}, s32[2,16]{1,0:T(2,128)}, u32[]{:S(2)}) copy-start(s32[2,16]{1,0:T(2,128)} %sx_ref.3) | copy-start | bytes 388
  0.0 1.6 %copy-start = (f32[16,16,16,128]{3,2,1,0:T(8,128)S(1)}, f32[16,16,16,128]{3,2,1,0:T(8,128)}, u32[]{:S(2)}) copy-start(f32[16,16,16,128]{3,2,1,0:T(8,128)} %param.10) | copy-start | bytes 6291460
  2.3 0.7 %copy-start.11 = (s32[2,16]{1,0:T(2,128)S(1)}, s32[2,16]{1,0:T(2,128)}, u32[]{:S(2)}) copy-start(s32[2,16]{1,0:T(2,128)} %sy_ref.3) | copy-start | bytes 388
  3.6 11.7 %copy-start.6 = (f32[3,18]{1,0:T(4,128)S(1)}, f32[3,18]{1,0:T(4,128)}, u32[]{:S(2)}) copy-start(f32[3,18]{1,0:T(4,128)} %lam_ref.3) | copy-start | bytes 652
  3.6 16.1 %copy-start.1 = (f32[16,16,16,128]{3,2,1,0:T(8,128)S(1)}, f32[16,16,16,128]{3,2,1,0:T(8,128)}, u32[]{:S(2)}) copy-start(f32[16,16,16,128]{3,2,1,0:T(8,128)} %param.10) | copy-start | bytes 6291460
  3.7 16.1 %copy-start.3 = (s32[6,128]{1,0:T(8,128)S(1)}, s32[6,128]{1,0:T(8,128)}, u32[]{:S(2)}) copy-start(s32[6,128]{1,0:T(8,128)} %src_ref.3) | copy-start | bytes 9220
  3.7 16.1 %copy-start.4 = (s32[6,128]{1,0:T(8,128)S(1)}, s32[6,128]{1,0:T(8,128)}, u32[]{:S(2)}) copy-start(s32[6,128]{1,0:T(8,128)} %idx_ref.3) | copy-start | bytes 9220
  3.7 16.1 %copy-start.5 = (s32[6,128]{1,0:T(8,128)S(1)}, s32[6,128]{1,0:T(8,128)}, u32[]{:S(2)}) copy-start(s32[6,128]{1,0:T(8,128)} %code_ref.3) | copy-start | bytes 9220
  4.4 15.2 %collective-permute-start.4 = (f32[128,128]{1,0:T(8,128)S(1)}, f32[128,128]{1,0:T(8,128)S(1)}, u32[]{:S(2)}, u32[]{:S(2)}) collective-permute-start(f32[128,128]{1,0:T(8,128)S(1)} %get-tuple-element.35), channel_id=1, source_target_pairs={{0,16},{1,17},{2,18},{3,19},{4,20},{5,21},{6,22},{7,23},{8,24},{9,... | collective-permute-start | bytes 196616 | tf_op jit(solution)/shard_map/ppermute | solution.py:312
  6.1 13.6 %collective-permute-start.5 = (f32[128,128]{1,0:T(8,128)S(1)}, f32[128,128]{1,0:T(8,128)S(1)}, u32[]{:S(2)}, u32[]{:S(2)}) collective-permute-start(f32[128,128]{1,0:T(8,128)S(1)} %get-tuple-element.36), channel_id=1, source_target_pairs={{0,1},{1,0},{2,3},{3,2},{4,5},{5,4},{6,7},{7,6},{8,9},{9,8},{10,11... | collective-permute-start | bytes 196616 | tf_op jit(solution)/shard_map/ppermute | solution.py:312
  8.2 2.0 %collective-permute-start = (f32[32,128]{1,0:T(8,128)S(1)}, f32[32,128]{1,0:T(8,128)S(1)}, u32[]{:S(2)}, u32[]{:S(2)}) collective-permute-start(f32[32,128]{1,0:T(8,128)S(1)} %get-tuple-element.31), channel_id=1, source_target_pairs={{0,1},{1,0},{2,3},{3,2},{4,5},{5,4},{6,7},{7,6},{8,9},{9,8},{10,11... | collective-permute-start | bytes 49160 | tf_op jit(solution)/shard_map/ppermute | solution.py:312
  8.2 11.4 %collective-permute-start.1 = (f32[32,128]{1,0:T(8,128)S(1)}, f32[32,128]{1,0:T(8,128)S(1)}, u32[]{:S(2)}, u32[]{:S(2)}) collective-permute-start(f32[32,128]{1,0:T(8,128)S(1)} %get-tuple-element.32), channel_id=1, source_target_pairs={{0,3},{1,2},{2,1},{3,0},{4,7},{5,6},{6,5},{7,4},{8,11},{9,10},{10,... | collective-permute-start | bytes 49160 | tf_op jit(solution)/shard_map/ppermute | solution.py:312
  10.3 9.4 %collective-permute-start.2 = (f32[32,128]{1,0:T(8,128)S(1)}, f32[32,128]{1,0:T(8,128)S(1)}, u32[]{:S(2)}, u32[]{:S(2)}) collective-permute-start(f32[32,128]{1,0:T(8,128)S(1)} %get-tuple-element.33), channel_id=1, source_target_pairs={{0,4},{1,5},{2,6},{3,7},{4,0},{5,1},{6,2},{7,3},{8,12},{9,13},{10,... | collective-permute-start | bytes 49160 | tf_op jit(solution)/shard_map/ppermute | solution.py:312
  10.3 9.4 %collective-permute-start.3 = (f32[32,128]{1,0:T(8,128)S(1)}, f32[32,128]{1,0:T(8,128)S(1)}, u32[]{:S(2)}, u32[]{:S(2)}) collective-permute-start(f32[32,128]{1,0:T(8,128)S(1)} %get-tuple-element.34), channel_id=1, source_target_pairs={{0,1},{1,0},{2,3},{3,2},{4,8},{5,9},{6,10},{7,11},{8,4},{9,5},{10,... | collective-permute-start | bytes 49160 | tf_op jit(solution)/shard_map/ppermute | solution.py:312
  15.3 0.8 %copy-start.2 = (f32[3,18,18]{2,1,0:T(8,128)S(1)}, f32[3,18,18]{2,1,0:T(8,128)}, u32[]{:S(2)}) copy-start(f32[3,18,18]{2,1,0:T(8,128)} %s_ref.1) | copy-start | bytes 11668
  16.1 0.7 %copy-start.7 = (f32[3,128]{1,0:T(4,128)S(1)}, f32[3,128]{1,0:T(4,128)}, u32[]{:S(2)}) copy-start(f32[3,128]{1,0:T(4,128)} %coeff_ref.3) | copy-start | bytes 4612
  19.7 0.7 %copy-start.8 = (f32[3,128]{1,0:T(4,128)S(1)}, f32[3,128]{1,0:T(4,128)}, u32[]{:S(2)}) copy-start(f32[3,128]{1,0:T(4,128)} %coeff_ref.3) | copy-start | bytes 4612
  20.4 0.7 %copy-start.12 = (s32[2,16]{1,0:T(2,128)S(1)}, s32[2,16]{1,0:T(2,128)}, u32[]{:S(2)}) copy-start(s32[2,16]{1,0:T(2,128)} %sy_ref.3) | copy-start | bytes 388
  28.8 9.4 %collective-permute-start.10 = (f32[128,128]{1,0:T(8,128)S(1)}, f32[128,128]{1,0:T(8,128)S(1)}, u32[]{:S(2)}, u32[]{:S(2)}) collective-permute-start(f32[128,128]{1,0:T(8,128)S(1)} %get-tuple-element.43), channel_id=1, source_target_pairs={{0,16},{1,17},{2,18},{3,19},{4,20},{5,21},{6,22},{7,23},{8,24},{9,... | collective-permute-start | bytes 196616 | tf_op jit(solution)/shard_map/ppermute | solution.py:312
  29.8 8.4 %collective-permute-start.11 = (f32[128,128]{1,0:T(8,128)S(1)}, f32[128,128]{1,0:T(8,128)S(1)}, u32[]{:S(2)}, u32[]{:S(2)}) collective-permute-start(f32[128,128]{1,0:T(8,128)S(1)} %get-tuple-element.44), channel_id=1, source_target_pairs={{0,1},{1,0},{2,3},{3,2},{4,5},{5,4},{6,7},{7,6},{8,9},{9,8},{10,11... | collective-permute-start | bytes 196616 | tf_op jit(solution)/shard_map/ppermute | solution.py:312
  31.2 1.2 %collective-permute-start.6 = (f32[32,128]{1,0:T(8,128)S(1)}, f32[32,128]{1,0:T(8,128)S(1)}, u32[]{:S(2)}, u32[]{:S(2)}) collective-permute-start(f32[32,128]{1,0:T(8,128)S(1)} %get-tuple-element.39), channel_id=1, source_target_pairs={{0,1},{1,0},{2,3},{3,2},{4,5},{5,4},{6,7},{7,6},{8,9},{9,8},{10,11... | collective-permute-start | bytes 49160 | tf_op jit(solution)/shard_map/ppermute | solution.py:312
  31.2 3.2 %collective-permute-start.7 = (f32[32,128]{1,0:T(8,128)S(1)}, f32[32,128]{1,0:T(8,128)S(1)}, u32[]{:S(2)}, u32[]{:S(2)}) collective-permute-start(f32[32,128]{1,0:T(8,128)S(1)} %get-tuple-element.40), channel_id=1, source_target_pairs={{0,3},{1,2},{2,1},{3,0},{4,7},{5,6},{6,5},{7,4},{8,11},{9,10},{10,... | collective-permute-start | bytes 49160 | tf_op jit(solution)/shard_map/ppermute | solution.py:312
  32.3 4.6 %collective-permute-start.8 = (f32[32,128]{1,0:T(8,128)S(1)}, f32[32,128]{1,0:T(8,128)S(1)}, u32[]{:S(2)}, u32[]{:S(2)}) collective-permute-start(f32[32,128]{1,0:T(8,128)S(1)} %get-tuple-element.41), channel_id=1, source_target_pairs={{0,4},{1,5},{2,6},{3,7},{4,0},{5,1},{6,2},{7,3},{8,12},{9,13},{10,... | collective-permute-start | bytes 49160 | tf_op jit(solution)/shard_map/ppermute | solution.py:312
  32.4 5.8 %collective-permute-start.9 = (f32[32,128]{1,0:T(8,128)S(1)}, f32[32,128]{1,0:T(8,128)S(1)}, u32[]{:S(2)}, u32[]{:S(2)}) collective-permute-start(f32[32,128]{1,0:T(8,128)S(1)} %get-tuple-element.42), channel_id=1, source_target_pairs={{0,1},{1,0},{2,3},{3,2},{4,8},{5,9},{6,10},{7,11},{8,4},{9,5},{10,... | collective-permute-start | bytes 49160 | tf_op jit(solution)/shard_map/ppermute | solution.py:312
  (3 other events, 2.0 us)

commit v2 on v1

v2 whole, which is shorter than its diff:
```python
import jax
import jax.numpy as jnp
from jax import lax
from jax.experimental import pallas as pl
from jax.experimental.pallas import tpu as pltpu
from jax.sharding import PartitionSpec as P


DEV_X = 4
DEV_Y = 4
ORDERS = ((5, 4, 0, 1, 2, 3), (5, 4, 0, 1, 2, 3))
NP = 16
NE = 18
PLANE = NP * NP
LANES = 128
WIDE = 336
NARROW = PLANE + 4 * NP
CHUNK = 8
DEEP = NE * CHUNK
F32 = jnp.float32
BF16 = jnp.bfloat16


def swap_pairs(axis, turn, size):
    layout = (DEV_X, DEV_Y, size // (DEV_X * DEV_Y))
    stride = (1, DEV_X, DEV_X * DEV_Y)[axis]
    pairs = []
    for i in range(size):
        place = i // stride % layout[axis]
        other = place + 1 if place % 2 == turn else place - 1
        if 0 <= other < layout[axis]:
            pairs.append((i, i + (other - place) * stride))
        else:
            pairs.append((i, i ^ (DEV_X - 1 if axis == 0 else 1)))
    return pairs


def odd_place(axis):
    stride = (1, DEV_X, DEV_X * DEV_Y)[axis]
    return (lax.axis_index("dev") // stride) % 2 == 1


def lane_take(values, index):
    return jnp.take_along_axis(values, index, axis=1, mode="promise_in_bounds")


def lanes(shape):
    return lax.broadcasted_iota(jnp.int32, shape, 1)


def block_ids(table, odd):
    first = jnp.where(odd, table[0:1], table[1:2])
    second = jnp.where(odd, table[1:2], table[0:1])
    repeats = LANES // table.shape[1] // 2
    return [jnp.concatenate(pair * repeats, axis=1) for pair in ([first, second], [second, first])]


def pack_axis(axis, plane, ids, count, first_ref, second_ref):
    blocks = LANES // count
    rows = PLANE // blocks
    patterns = []
    for row in ids:
        row = jnp.broadcast_to(row, (8, LANES))
        patterns.append((row & (LANES - 1), (row // LANES) == 2 * axis + 1))
    lane_block = lanes((8, LANES)) // count
    for row in range(0, rows, 8):
        first_value = jnp.zeros((8, LANES), F32)
        second_value = jnp.zeros((8, LANES), F32)
        for block in range(blocks):
            slot, is_high = patterns[block % 2]
            start = block * rows + row
            got = jnp.where(is_high, lane_take(plane(1, start), slot), lane_take(plane(0, start), slot))
            first_value = jnp.where(lane_block == block, got, first_value)
            second_value = jnp.where(lane_block == block ^ 1, got, second_value)
        first_ref[row : row + 8] = first_value
        second_ref[row : row + 8] = second_value


def local_face(face, plane, source, index, put):
    axis = face // 2
    full = lambda row: jnp.broadcast_to(row, (8, LANES))
    source, index = full(source), full(index)
    slot = index & (LANES - 1)
    local = source == 1
    high = (index // LANES) == 2 * axis + 1
    for start in range(0, PLANE, 8):
        here = jnp.where(high, lane_take(plane(1, start), slot), lane_take(plane(0, start), slot))
        put(start, jnp.where(local, here, 0.0))


def unpack_face(face, local, odd, first_ref, second_ref, source, index, code):
    axis = face // 2
    rows = first_ref.shape[0]
    blocks = PLANE // rows
    count = LANES // blocks
    full = lambda row: jnp.broadcast_to(row, (8, LANES))
    source, index, code = full(source), full(index), full(code)
    from_first = source == jnp.where(odd, 3 + 2 * axis, 2 + 2 * axis)
    from_second = source == jnp.where(odd, 2 + 2 * axis, 3 + 2 * axis)
    position = index & (count - 1)
    flip_first = (code & 1) == 1
    flip_second = (code & 2) == 2
    reverse = 7 - lax.broadcasted_iota(jnp.int32, (8, LANES), 0)

    def fetch(start):
        block, row = start // rows, start % rows
        one = lane_take(first_ref[row : row + 8], position + block * count)
        two = lane_take(second_ref[row : row + 8], position + (block ^ 1) * count)
        return jnp.where(from_first, one, jnp.where(from_second, two, local(start)))

    def turn(value):
        return jnp.take_along_axis(value, reverse, axis=0, mode="promise_in_bounds")

    def lines(p):
        q = NP - 1 - p
        pieces = [[fetch(line * NP), fetch(line * NP + 8)] for line in (p, q)]
        result = []
        for line, near, far in ((p, pieces[0], pieces[1]), (q, pieces[1], pieces[0])):
            first = [jnp.where(flip_first, far[h], near[h]) for h in range(2)]
            result.append((line, [jnp.where(flip_second, turn(first[1 - h]), first[h]) for h in range(2)]))
        return result

    return lines


def field_plane(field_ref, axis):
    def plane(side, start):
        layer = 1 if side == 0 else NP - 2
        if axis == 0:
            return field_ref[layer * PLANE + start : layer * PLANE + start + 8]
        if axis == 1:
            base = (start // NP) * PLANE + layer * NP + start % NP
            return field_ref[base : base + 8]
        return field_ref[pl.ds(start * NP + layer, 8, stride=NP)]

    return plane


def rim_plane(rim_ref, axis):
    def plane(side, start):
        base = (2 * axis + side) * PLANE + start
        return rim_ref[base : base + 8]

    return plane


def pack_kernel(field_ref, table_ref, o0, o1, o2, o3, o4, o5, ids_ref):
    outs = (o0, o1, o2, o3, o4, o5)
    start = 0
    for axis in range(3):
        count = LANES * outs[2 * axis].shape[0] // PLANE
        patterns = block_ids(table_ref[:, start : start + count], odd_place(axis))
        start += count
        for half in range(2):
            ids_ref[2 * axis + half : 2 * axis + half + 1] = patterns[half]
        pack_axis(axis, field_plane(field_ref, axis), patterns, count, outs[2 * axis], outs[2 * axis + 1])


def split(value):
    high = value.astype(BF16)
    return high, (value - high.astype(F32)).astype(BF16)


def stacked(value):
    high, low = split(value)
    return jnp.concatenate([high, high, low], axis=0)


def operator(value):
    high, low = split(value)
    return jnp.concatenate([high, low, high], axis=1)


def exact_dot(a, b):
    return jnp.dot(a, b, precision=lax.Precision.HIGHEST, preferred_element_type=F32)


def write_operators(s_ref, lam_ref, coeff_ref, main_ref, rim_ref, back_ref, to_ref, from_ref, base_ref, edge_ref):
    iota = lambda shape, dim: lax.broadcasted_iota(jnp.int32, shape, dim)

    def node(kidx, small_first):
        inner = kidx < PLANE
        t = kidx - PLANE
        group = t // NP
        along = 1 + t % NP
        if small_first:
            return jnp.where(inner, 1 + kidx // NP, jnp.where(group == 0, 0, jnp.where(group == 1, NE - 1, along)))
        return jnp.where(inner, 1 + kidx % NP, jnp.where(group == 2, 0, jnp.where(group == 3, NE - 1, along)))

    def hot(cond):
        return jnp.where(cond, 1.0, 0.0).astype(F32)

    wide_b = hot(iota((WIDE, NE), 0) // NE == iota((WIDE, NE), 1))
    wide_c = hot((iota((WIDE, NE), 0) % NE == iota((WIDE, NE), 1)) & (iota((WIDE, NE), 0) < NE * NE))
    wide_bt = hot(iota((NE, WIDE), 1) // NE == iota((NE, WIDE), 0))
    wide_ct = hot((iota((NE, WIDE), 1) % NE == iota((NE, WIDE), 0)) & (iota((NE, WIDE), 1) < NE * NE))
    node_j = hot(node(iota((NARROW, NE), 0), True) == iota((NARROW, NE), 1))
    node_k = hot(node(iota((NARROW, NE), 0), False) == iota((NARROW, NE), 1))
    node_jt = hot(node(iota((NE, NARROW), 1), True) == iota((NE, NARROW), 0))
    node_kt = hot(node(iota((NE, NARROW), 1), False) == iota((NE, NARROW), 0))
    s0, s1, s2 = s_ref[0], s_ref[1], s_ref[2]
    t0, t1, t2 = s0.T, s1.T, s2.T
    ahead = exact_dot(wide_b, exact_dot(t1, node_jt)) * exact_dot(wide_c, exact_dot(t2, node_kt))
    main_ref[...] = operator(ahead[:, :PLANE])
    rim_ref[...] = operator(ahead[:, PLANE:])
    back = exact_dot(node_j, exact_dot(s1, wide_bt)) * exact_dot(node_k, exact_dot(s2, wide_ct))
    back_ref[...] = operator(back)
    deep = hot(iota((DEEP, NE), 0) // CHUNK == iota((DEEP, NE), 1))
    deep_t = hot(iota((NE, DEEP), 1) // CHUNK == iota((NE, DEEP), 0))
    same = hot(iota((DEEP, DEEP), 0) % CHUNK == iota((DEEP, DEEP), 1) % CHUNK)
    to_ref[...] = operator(exact_dot(deep, exact_dot(t0, deep_t)) * same)
    from_ref[...] = operator(exact_dot(deep, exact_dot(s0, deep_t)) * same)
    col_b = jnp.sum(wide_b * lam_ref[1:2], axis=1, keepdims=True)
    col_c = jnp.sum(wide_c * lam_ref[2:3], axis=1, keepdims=True)
    base_ref[...] = col_b * coeff_ref[1:2] + col_c * coeff_ref[2:3]
    same_a = hot(iota((NE, NE), 0) == iota((NE, NE), 1))
    edge_ref[...] = jnp.sum(same_a * lam_ref[0:1], axis=1, keepdims=True) * coeff_ref[0:1]


def mm(a, b):
    return jnp.dot(a, b, preferred_element_type=F32)


def both(load):
    return jnp.concatenate([load(0), load(1)], axis=1)


def plane_rows(number, count=1):
    return slice(number * PLANE, (number + count) * PLANE)


def line_rows(face, line):
    return slice(face * PLANE + line * NP, face * PLANE + (line + 1) * NP)


def begin_kernel(
    field_ref, s_ref, lam_ref, coeff_ref, src_ref, idx_ref, code_ref,
    main_ref, rim_ref, back_ref, to_ref, from_ref, base_ref, edge_ref, table_ref, local_ref, work_ref,
):
    for n, ref in enumerate((src_ref, idx_ref, code_ref)):
        table_ref[n] = ref[...]
    write_operators(s_ref, lam_ref, coeff_ref, main_ref, rim_ref, back_ref, to_ref, from_ref, base_ref, edge_ref)
    for face in range(6):
        def put(start, value, face=face):
            local_ref[face * PLANE + start : face * PLANE + start + 8] = value

        local_face(
            face, field_plane(field_ref, face // 2), table_ref[0, face : face + 1], table_ref[1, face : face + 1], put
        )
    for pair in range(NP // 2):
        got = mm(main_ref[...], stacked(both(lambda s: field_ref[plane_rows(2 * pair + s)])))
        for s in range(2):
            work_ref[2 * pair + s] = got[:, s * LANES : (s + 1) * LANES]


def faces(local_ref, table_ref, messages):
    result = []
    for face in range(6):
        def local(start, face=face):
            return local_ref[face * PLANE + start : face * PLANE + start + 8]

        axis = face // 2
        rows = [table_ref[n, face : face + 1] for n in range(3)]
        result.append(unpack_face(face, local, odd_place(axis), messages[2 * axis], messages[2 * axis + 1], *rows))
    return result


def middle_kernel(
    local_ref, table_ref, ids_ref, first_ref, main_ref, rim_op_ref, back_ref, to_ref, from_ref, base_ref, edge_ref,
    m0, m1, m2, m3, m4, m5,
    work_ref, rim_ref, o0, o1, o2, o3, o4, o5,
    ghost_ref,
):
    outs = (o0, o1, o2, o3, o4, o5)
    for face, lines in enumerate(faces(local_ref, table_ref, (m0, m1, m2, m3, m4, m5))):
        for p in range(NP // 2):
            for line, pieces in lines(p):
                for h in range(2):
                    ghost_ref[pl.ds(face * PLANE + line * NP + 8 * h, 8)] = pieces[h]

    got = mm(main_ref[...], stacked(both(lambda s: ghost_ref[plane_rows(s)])))
    work_ref[0] = got[:, :LANES]
    work_ref[NE - 1] = got[:, LANES:]
    for pair in range(NP // 2):
        sides = [both(lambda s: ghost_ref[line_rows(f, 2 * pair + s)]) for f in range(2, 6)]
        got = mm(rim_op_ref[...], stacked(jnp.concatenate(sides, axis=0)))
        for s in range(2):
            i = 2 * pair + s
            work_ref[1 + i] = first_ref[i] + got[:, s * LANES : (s + 1) * LANES]

    for step in range(WIDE // CHUNK // 2):
        rows = [slice((2 * step + s) * CHUNK, (2 * step + s + 1) * CHUNK) for s in range(2)]
        chunk = both(lambda s: work_ref[:, rows[s], :].reshape(DEEP, LANES))
        coef = mm(to_ref[...], stacked(chunk))
        divisor = both(
            lambda s: jnp.concatenate([edge_ref[a : a + 1] + base_ref[rows[s], :] for a in range(NE)], axis=0)
        )
        solved = mm(from_ref[...], stacked(coef / divisor))
        for s in range(2):
            work_ref[:, rows[s], :] = solved[:, s * LANES : (s + 1) * LANES].reshape(NE, CHUNK, LANES)

    got = mm(back_ref[:PLANE], stacked(both(lambda s: work_ref[s * (NE - 1)])))
    rim_ref[plane_rows(0)] = got[:, :LANES]
    rim_ref[plane_rows(1)] = got[:, LANES:]
    for pair in range(NP // 2):
        got = mm(back_ref[PLANE:], stacked(both(lambda s: work_ref[1 + 2 * pair + s])))
        for s in range(2):
            for f in range(2, 6):
                rim_ref[line_rows(f, 2 * pair + s)] = got[(f - 2) * NP : (f - 1) * NP, s * LANES : (s + 1) * LANES]
    for axis in range(3):
        ids = [ids_ref[2 * axis + half : 2 * axis + half + 1] for half in range(2)]
        count = LANES * outs[2 * axis].shape[0] // PLANE
        pack_axis(axis, rim_plane(rim_ref, axis), ids, count, outs[2 * axis], outs[2 * axis + 1])


def inside_kernel(work_ref, back_ref, rim_ref, table_ref, inner_ref, local_ref):
    for pair in range(NP // 2):
        got = mm(back_ref[:PLANE], stacked(both(lambda s: work_ref[1 + 2 * pair + s])))
        for s in range(2):
            inner_ref[plane_rows(2 * pair + s)] = got[:, s * LANES : (s + 1) * LANES]
    for face in range(6):
        def put(start, value, face=face):
            local_ref[face * PLANE + start : face * PLANE + start + 8] = value

        local_face(face, rim_plane(rim_ref, face // 2), table_ref[0, face : face + 1], table_ref[1, face : face + 1], put)


def finish_kernel(inner_ref, local_ref, table_ref, m0, m1, m2, m3, m4, m5, out_hbm, out_ref, sems):
    sides = faces(local_ref, table_ref, (m0, m1, m2, m3, m4, m5))

    def add(place, value):
        out_ref[place] = out_ref[place] + value

    copies = []
    out_ref[plane_rows(1)] = inner_ref[plane_rows(1)]
    out_ref[plane_rows(NP - 2)] = inner_ref[plane_rows(NP - 2)]
    for face, layer in ((0, 1), (1, NP - 2)):
        for p in range(NP // 2):
            for line, pieces in sides[face](p):
                for h in range(2):
                    add(pl.ds(layer * PLANE + line * NP + 8 * h, 8), pieces[h])
    for p in range(NP // 2):
        for i in (p, NP - 1 - p):
            if i not in (1, NP - 2):
                out_ref[plane_rows(i)] = inner_ref[plane_rows(i)]
        for face in range(2, 6):
            layer = 1 if face % 2 == 0 else NP - 2
            for line, pieces in sides[face](p):
                for h in range(2):
                    if face < 4:
                        add(pl.ds(line * PLANE + layer * NP + 8 * h, 8), pieces[h])
                    else:
                        add(pl.ds((line * NP + 8 * h) * NP + layer, 8, stride=NP), pieces[h])
        for i in (p, NP - 1 - p):
            rows = plane_rows(i)
            copies.append(pltpu.make_async_copy(out_ref.at[rows], out_hbm.at[rows], sems.at[i]))
            copies[-1].start()
    for copy in copies:
        copy.wait()


VMEM = pl.BlockSpec(memory_space=pltpu.VMEM)
HBM = pl.BlockSpec(memory_space=pltpu.HBM)


def grant(mebibytes):
    return pltpu.CompilerParams(vmem_limit_bytes=mebibytes << 20)


def message_shapes(tables):
    shapes = []
    for table in tables:
        rows = PLANE * table.shape[1] // LANES
        shapes += [jax.ShapeDtypeStruct((rows, LANES), F32)] * 2
    return shapes


def exchange(messages, phase):
    arrived = [None] * 6
    for number in ORDERS[phase]:
        pairs = swap_pairs(number // 2, number % 2, lax.axis_size("dev"))
        arrived[number] = lax.ppermute(messages[number], "dev", pairs)
    return arrived


def shards(field, s_mats, lam, coeff, nbr_src, nbr_idx, orient, send_x, send_y, send_z):
    flat = field.reshape(NP * PLANE, LANES)
    tables = (send_x, send_y, send_z)
    shape = jax.ShapeDtypeStruct
    planes = shape((6 * PLANE, LANES), F32)
    block = shape((NP * PLANE, LANES), F32)
    packed = pl.pallas_call(
        pack_kernel, out_shape=message_shapes(tables) + [shape((8, LANES), jnp.int32)],
        in_specs=[VMEM] * 2, out_specs=[VMEM] * 7, compiler_params=grant(8), name="pack",
    )(flat, jnp.concatenate(tables, axis=1))
    outgoing, ids = packed[:6], packed[6]
    arrived = exchange(outgoing, 0)
    begun = pl.pallas_call(
        begin_kernel,
        out_shape=[
            shape((WIDE, 3 * PLANE), BF16), shape((WIDE, 12 * NP), BF16), shape((NARROW, 3 * WIDE), BF16),
            shape((DEEP, 3 * DEEP), BF16), shape((DEEP, 3 * DEEP), BF16), shape((WIDE, LANES), F32),
            shape((NE, LANES), F32), shape((3, 6, LANES), jnp.int32), planes, shape((NP, WIDE, LANES), F32),
        ],
        in_specs=[VMEM] * 7, out_specs=[VMEM] * 10,
        compiler_params=grant(20), name="begin",
        cost_estimate=pl.CostEstimate(flops=2 * 8 * WIDE * 1024 * 256, bytes_accessed=0, transcendentals=0),
    )(flat, s_mats, lam, coeff, nbr_src, nbr_idx, orient)
    operators, (table, local, first) = begun[:7], begun[7:]
    solved = pl.pallas_call(
        middle_kernel, out_shape=[shape((NE, WIDE, LANES), F32), planes] + message_shapes(tables),
        in_specs=[VMEM] * 17, out_specs=[VMEM] * 8, scratch_shapes=[pltpu.VMEM((6 * PLANE, LANES), F32)],
        compiler_params=grant(20), name="middle",
    )(local, table, ids, first, *operators, *arrived)
    work, rims = solved[:2]
    returned = exchange(solved[2:], 1)
    inner, local = pl.pallas_call(
        inside_kernel, out_shape=[block, planes], in_specs=[VMEM] * 4, out_specs=[VMEM] * 2,
        compiler_params=grant(16), name="inside",
        cost_estimate=pl.CostEstimate(flops=2 * 8 * PLANE * 1024 * 256, bytes_accessed=0, transcendentals=0),
    )(work, operators[2], rims, table)
    out = pl.pallas_call(
        finish_kernel, out_shape=block, in_specs=[VMEM] * 9, out_specs=HBM,
        scratch_shapes=[pltpu.VMEM(block.shape, F32), pltpu.SemaphoreType.DMA((NP,))],
        compiler_params=grant(12), name="finish",
    )(inner, local, table, *returned)
    return out.reshape(field.shape)


def solution(mesh):
    split_last = P(None, "dev")
    placed = (P(None, None, None, "dev"), P(), P()) + (split_last,) * 7
    return jax.shard_map(shards, mesh=mesh, in_specs=placed, out_specs=P(None, None, None, "dev"), check_vma=False)
```

time: 42 us -> 37.5 us (0.89)
  the two profiles are of different devices: /device:TPU:68 before, /device:TPU:2 now
where the time goes in v2:
time: 37.5 us; the launch traced here: 37.3 us
  starting transfers between devices  17.4 us (46%)
  Pallas kernels  12.6 us (34%)
  waiting for transfers between devices  3.72 us (10%)
  local copies, waits for them, and re-layouts  2.38 us (6%)
  other arithmetic  0.8 us (2%)
    ppermute x12, starting transfers between devices, exchange(): arrived[number] = lax.ppermute(messages[number], 'dev', pairs)  17.4 us
    pallas_call x1, Pallas kernels, shards(): pl.pallas_call(middle_kernel, out_shape=[shape((NE, WIDE, LANES), F32), p...  4.63 us
    pallas_call x1, Pallas kernels, shards(): pl.pallas_call(begin_kernel, out_shape=[shape((WIDE, 3 * PLANE), BF16), s...  4.01 us
    ppermute x12, waiting for transfers between devices, exchange(): arrived[number] = lax.ppermute(messages[number], 'dev', pairs)  3.72 us
    unnamed x16, local copies, waits for them, and re-layouts  2.38 us
    pallas_call x1, Pallas kernels, shards(): pl.pallas_call(finish_kernel, out_shape=block, in_specs=[VMEM] * 9, out_s...  1.93 us
    pallas_call x1, Pallas kernels, shards(): pl.pallas_call(inside_kernel, out_shape=[block, planes], in_specs=[VMEM]...  1.3 us
    concatenate x1, other arithmetic, shards(): jnp.concatenate(tables, axis=1)  0.8 us
  transfers between devices with their start and end apart: 12, of which 2 were waited for; matrix products, arithmetic and copies ran while one was open for 0% of the time, Pallas kernels for 14%

profile of v2, /device:TPU:2, one launch (start us, length us, event | category | flops | bytes accessed | tf_op | source)
XLA Modules:
  0.0 37.3 jit_solution(15608817404769790076)
XLA Ops:
  0.0 0.8 %pad_add_fusion.table_ref = s32[2,96]{1,0:T(2,128)S(1)} fusion(s32[2,64]{1,0:T(2,128)} %param.19, s32[2,16]{1,0:T(2,128)} %param.18, s32[2,16]{1,0:T(2,128)} %param.17), kind=kLoop, calls=%fused_computation | loop fusion | flops 384 | bytes 1536 | tf_op jit(solution)/shard_map/concatenate | solution.py:395
  0.8 1.6 %copy-done = f32[16,16,16,128]{3,2,1,0:T(8,128)S(1)} copy-done((f32[16,16,16,128]{3,2,1,0:T(8,128)S(1)}, f32[16,16,16,128]{3,2,1,0:T(8,128)}, u32[]{:S(2)}) %copy-start) | copy-done | bytes 2097176
  2.4 0.0 copy-start.7
  2.4 0.8 %pack.1 = (f32[32,128]{1,0:T(8,128)S(1)}, f32[32,128]{1,0:T(8,128)S(1)}, f32[32,128]{1,0:T(8,128)S(1)}, f32[32,128]{1,0:T(8,128)S(1)}, f32[128,128]{1,0:T(8,128)...) custom-call(f32[4096,128]{1,0:T(8,128)S(1)} %bitcast.2, s32[2,96]{1,0:T(2,128)S(1)} %pad_add_fusion.table_ref), custom_call_target="tpu_custom_call" | custom-call | tf_op jit(solution)/shard_map/pack/pallas_call | solution.py:392
  3.2 0.1 collective-permute-start
  3.3 2.0 %collective-permute-start.1 = (f32[32,128]{1,0:T(8,128)S(1)}, f32[32,128]{1,0:T(8,128)S(1)}, u32[]{:S(2)}, u32[]{:S(2)}) collective-permute-start(f32[32,128]{1,0:T(8,128)S(1)} %get-tuple-element.44), channel_id=1, source_target_pairs={{0,3},{1,2},{2,1},{3,0},{4,7},{5,6},{6,5},{7,4},{8,11},{9,10},{10,... | collective-permute-start | bytes 49160 | tf_op jit(solution)/shard_map/ppermute | solution.py:382
  5.3 3.3 %collective-permute-start.2 = (f32[32,128]{1,0:T(8,128)S(1)}, f32[32,128]{1,0:T(8,128)S(1)}, u32[]{:S(2)}, u32[]{:S(2)}) collective-permute-start(f32[32,128]{1,0:T(8,128)S(1)} %get-tuple-element.45), channel_id=1, source_target_pairs={{0,4},{1,5},{2,6},{3,7},{4,0},{5,1},{6,2},{7,3},{8,12},{9,13},{10,... | collective-permute-start | bytes 49160 | tf_op jit(solution)/shard_map/ppermute | solution.py:382
  8.6 0.0 collective-permute-start.3
  8.6 1.6 %collective-permute-start.4 = (f32[128,128]{1,0:T(8,128)S(1)}, f32[128,128]{1,0:T(8,128)S(1)}, u32[]{:S(2)}, u32[]{:S(2)}) collective-permute-start(f32[128,128]{1,0:T(8,128)S(1)} %get-tuple-element.47), channel_id=1, source_target_pairs={{0,16},{1,17},{2,18},{3,19},{4,20},{5,21},{6,22},{7,23},{8,24},{9,... | collective-permute-start | bytes 196616 | tf_op jit(solution)/shard_map/ppermute | solution.py:382
  10.1 0.0 collective-permute-done.m0
  10.2 2.2 %collective-permute-start.5 = (f32[128,128]{1,0:T(8,128)S(1)}, f32[128,128]{1,0:T(8,128)S(1)}, u32[]{:S(2)}, u32[]{:S(2)}) collective-permute-start(f32[128,128]{1,0:T(8,128)S(1)} %get-tuple-element.48), channel_id=1, source_target_pairs={{0,1},{1,0},{2,3},{3,2},{4,5},{5,4},{6,7},{7,6},{8,9},{9,8},{10,11... | collective-permute-start | bytes 196616 | tf_op jit(solution)/shard_map/ppermute | solution.py:382
  12.3 0.0 copy-start.2
  12.3 0.8 %copy-done.2 = f32[3,18,18]{2,1,0:T(8,128)S(1)} copy-done((f32[3,18,18]{2,1,0:T(8,128)S(1)}, f32[3,18,18]{2,1,0:T(8,128)}, u32[]{:S(2)}) %copy-start.2) | copy-done | bytes 3912
  13.1 4.0 %begin.1 = (bf16[336,768]{1,0:T(8,128)(2,1)S(1)}, bf16[336,192]{1,0:T(8,128)(2,1)S(1)}, bf16[320,1008]{1,0:T(8,128)(2,1)S(1)}, bf16[144,432]{1,0:T(8,128)(2,1)S(...) custom-call(f32[4096,128]{1,0:T(8,128)S(1)} %bitcast.3, ...), custom_call_target="tpu_custom_call" | custom-call | flops 1409286144 | tf_op jit(solution)/shard_map/begin/pallas_call | solution.py:398
  17.2 4.6 %middle.1 = (f32[18,336,128]{2,1,0:T(8,128)S(1)}, f32[1536,128]{1,0:T(8,128)S(1)}, f32[32,128]{1,0:T(8,128)S(1)}, f32[32,128]{1,0:T(8,128)S(1)}, f32[32,128]{1,0...) custom-call(f32[1536,128]{1,0:T(8,128)S(1)} %get-tuple-element.32.local_ref, ...), custom_call_target="tpu_custom_call" | custom-call | tf_op jit(solution)/shard_map/middle/pallas_call | solution.py:410
  21.8 0.1 collective-permute-start.6
  21.9 0.3 collective-permute-start.7
  22.2 5.9 %collective-permute-start.8 = (f32[32,128]{1,0:T(8,128)S(1)}, f32[32,128]{1,0:T(8,128)S(1)}, u32[]{:S(2)}, u32[]{:S(2)}) collective-permute-start(f32[32,128]{1,0:T(8,128)S(1)} %get-tuple-element.55), channel_id=1, source_target_pairs={{0,4},{1,5},{2,6},{3,7},{4,0},{5,1},{6,2},{7,3},{8,12},{9,13},{10,... | collective-permute-start | bytes 49160 | tf_op jit(solution)/shard_map/ppermute | solution.py:382
  28.1 0.7 %collective-permute-start.10 = (f32[128,128]{1,0:T(8,128)S(1)}, f32[128,128]{1,0:T(8,128)S(1)}, u32[]{:S(2)}, u32[]{:S(2)}) collective-permute-start(f32[128,128]{1,0:T(8,128)S(1)} %get-tuple-element.57), channel_id=1, source_target_pairs={{0,16},{1,17},{2,18},{3,19},{4,20},{5,21},{6,22},{7,23},{8,24},{9,... | collective-permute-start | bytes 196616 | tf_op jit(solution)/shard_map/ppermute | solution.py:382
  28.8 1.3 %collective-permute-start.11 = (f32[128,128]{1,0:T(8,128)S(1)}, f32[128,128]{1,0:T(8,128)S(1)}, u32[]{:S(2)}, u32[]{:S(2)}) collective-permute-start(f32[128,128]{1,0:T(8,128)S(1)} %get-tuple-element.58), channel_id=1, source_target_pairs={{0,1},{1,0},{2,3},{3,2},{4,5},{5,4},{6,7},{7,6},{8,9},{9,8},{10,11... | collective-permute-start | bytes 196616 | tf_op jit(solution)/shard_map/ppermute | solution.py:382
  30.1 1.3 %inside.1 = (f32[4096,128]{1,0:T(8,128)S(1)}, f32[1536,128]{1,0:T(8,128)S(1)}) custom-call(f32[18,336,128]{2,1,0:T(8,128)S(1)} %get-tuple-element.49.work_ref, bf16[320,1008]{1,0:T(8,128)(2,1)S(1)} %get-tuple-element.38.back_ref, f32[1536,128]{1,0:T(8,128)S(1)} %get-tuple-element.50.rim_ref, s32[3,6,128]{2,1,0:T(8,128)S(1)} %get-tuple-element.33.table_ref), custom_call_target="tpu_custom_call" | custom-call | flops 1073741824 | tf_op jit(solution)/shard_map/inside/pallas_call | solution.py:417
  31.5 1.1 %collective-permute-done.10.m4 = f32[128,128]{1,0:T(8,128)S(1)} collective-permute-done((f32[128,128]{1,0:T(8,128)S(1)}, f32[128,128]{1,0:T(8,128)S(1)}, u32[]{:S(2)}, u32[]{:S(2)}) %collective-permute-start.10) | collective-permute-done | bytes 65568 | tf_op jit(solution)/shard_map/ppermute | solution.py:382
  32.6 2.6 %collective-permute-done.11.m5 = f32[128,128]{1,0:T(8,128)S(1)} collective-permute-done((f32[128,128]{1,0:T(8,128)S(1)}, f32[128,128]{1,0:T(8,128)S(1)}, u32[]{:S(2)}, u32[]{:S(2)}) %collective-permute-start.11) | collective-permute-done | bytes 65568 | tf_op jit(solution)/shard_map/ppermute | solution.py:382
  35.2 1.9 %finish.1 = f32[4096,128]{1,0:T(8,128)} custom-call(f32[4096,128]{1,0:T(8,128)S(1)} %get-tuple-element.51.inner_ref, f32[1536,128]{1,0:T(8,128)S(1)} %get-tuple-element.52.local_ref, s32[3,6,128]{2,1,0:T(8,128)S(1)} %get-tuple-element.33.table_ref, f32[32,128]{1,0:T(8,128)S(1)} %collective-permute-done.6.m0, f32[32,128]{1,0:T(8,128)S(1)} %collective-permute-done.7.m1, ...), custom_call_target="tpu_custom_call" | custom-call | tf_op jit(solution)/shard_map/finish/pallas_call | solution.py:422
  (22 shorter events, 0.0 us)
Async XLA Ops:
  0.0 12.3 %copy-start.3 = (s32[6,128]{1,0:T(8,128)S(1)}, s32[6,128]{1,0:T(8,128)}, u32[]{:S(2)}) copy-start(s32[6,128]{1,0:T(8,128)} %src_ref.1) | copy-start | bytes 9220
  0.8 1.6 %copy-start = (f32[16,16,16,128]{3,2,1,0:T(8,128)S(1)}, f32[16,16,16,128]{3,2,1,0:T(8,128)}, u32[]{:S(2)}) copy-start(f32[16,16,16,128]{3,2,1,0:T(8,128)} %param.10) | copy-start | bytes 6291460
  2.4 9.9 %copy-start.1 = (f32[16,16,16,128]{3,2,1,0:T(8,128)S(1)}, f32[16,16,16,128]{3,2,1,0:T(8,128)}, u32[]{:S(2)}) copy-start(f32[16,16,16,128]{3,2,1,0:T(8,128)} %param.10) | copy-start | bytes 6291460
  2.4 9.9 %copy-start.4 = (s32[6,128]{1,0:T(8,128)S(1)}, s32[6,128]{1,0:T(8,128)}, u32[]{:S(2)}) copy-start(s32[6,128]{1,0:T(8,128)} %idx_ref.1) | copy-start | bytes 9220
  2.4 9.9 %copy-start.5 = (s32[6,128]{1,0:T(8,128)S(1)}, s32[6,128]{1,0:T(8,128)}, u32[]{:S(2)}) copy-start(s32[6,128]{1,0:T(8,128)} %code_ref.1) | copy-start | bytes 9220
  2.4 9.9 %copy-start.6 = (f32[3,18]{1,0:T(4,128)S(1)}, f32[3,18]{1,0:T(4,128)}, u32[]{:S(2)}) copy-start(f32[3,18]{1,0:T(4,128)} %lam_ref.1) | copy-start | bytes 652
  2.4 9.9 %copy-start.7 = (f32[3,128]{1,0:T(4,128)S(1)}, f32[3,128]{1,0:T(4,128)}, u32[]{:S(2)}) copy-start(f32[3,128]{1,0:T(4,128)} %coeff_ref.1) | copy-start | bytes 4612
  3.2 7.0 %collective-permute-start = (f32[32,128]{1,0:T(8,128)S(1)}, f32[32,128]{1,0:T(8,128)S(1)}, u32[]{:S(2)}, u32[]{:S(2)}) collective-permute-start(f32[32,128]{1,0:T(8,128)S(1)} %get-tuple-element.43), channel_id=1, source_target_pairs={{0,1},{1,0},{2,3},{3,2},{4,5},{5,4},{6,7},{7,6},{8,9},{9,8},{10,11... | collective-permute-start | bytes 49160 | tf_op jit(solution)/shard_map/ppermute | solution.py:382
  3.3 13.9 %collective-permute-start.1 = (f32[32,128]{1,0:T(8,128)S(1)}, f32[32,128]{1,0:T(8,128)S(1)}, u32[]{:S(2)}, u32[]{:S(2)}) collective-permute-start(f32[32,128]{1,0:T(8,128)S(1)} %get-tuple-element.44), channel_id=1, source_target_pairs={{0,3},{1,2},{2,1},{3,0},{4,7},{5,6},{6,5},{7,4},{8,11},{9,10},{10,... | collective-permute-start | bytes 49160 | tf_op jit(solution)/shard_map/ppermute | solution.py:382
  5.3 11.8 %collective-permute-start.2 = (f32[32,128]{1,0:T(8,128)S(1)}, f32[32,128]{1,0:T(8,128)S(1)}, u32[]{:S(2)}, u32[]{:S(2)}) collective-permute-start(f32[32,128]{1,0:T(8,128)S(1)} %get-tuple-element.45), channel_id=1, source_target_pairs={{0,4},{1,5},{2,6},{3,7},{4,0},{5,1},{6,2},{7,3},{8,12},{9,13},{10,... | collective-permute-start | bytes 49160 | tf_op jit(solution)/shard_map/ppermute | solution.py:382
  8.6 8.6 %collective-permute-start.3 = (f32[32,128]{1,0:T(8,128)S(1)}, f32[32,128]{1,0:T(8,128)S(1)}, u32[]{:S(2)}, u32[]{:S(2)}) collective-permute-start(f32[32,128]{1,0:T(8,128)S(1)} %get-tuple-element.46), channel_id=1, source_target_pairs={{0,1},{1,0},{2,3},{3,2},{4,8},{5,9},{6,10},{7,11},{8,4},{9,5},{10,... | collective-permute-start | bytes 49160 | tf_op jit(solution)/shard_map/ppermute | solution.py:382
  8.6 8.6 %collective-permute-start.4 = (f32[128,128]{1,0:T(8,128)S(1)}, f32[128,128]{1,0:T(8,128)S(1)}, u32[]{:S(2)}, u32[]{:S(2)}) collective-permute-start(f32[128,128]{1,0:T(8,128)S(1)} %get-tuple-element.47), channel_id=1, source_target_pairs={{0,16},{1,17},{2,18},{3,19},{4,20},{5,21},{6,22},{7,23},{8,24},{9,... | collective-permute-start | bytes 196616 | tf_op jit(solution)/shard_map/ppermute | solution.py:382
  10.2 7.0 %collective-permute-start.5 = (f32[128,128]{1,0:T(8,128)S(1)}, f32[128,128]{1,0:T(8,128)S(1)}, u32[]{:S(2)}, u32[]{:S(2)}) collective-permute-start(f32[128,128]{1,0:T(8,128)S(1)} %get-tuple-element.48), channel_id=1, source_target_pairs={{0,1},{1,0},{2,3},{3,2},{4,5},{5,4},{6,7},{7,6},{8,9},{9,8},{10,11... | collective-permute-start | bytes 196616 | tf_op jit(solution)/shard_map/ppermute | solution.py:382
  12.3 0.8 %copy-start.2 = (f32[3,18,18]{2,1,0:T(8,128)S(1)}, f32[3,18,18]{2,1,0:T(8,128)}, u32[]{:S(2)}) copy-start(f32[3,18,18]{2,1,0:T(8,128)} %s_ref.1) | copy-start | bytes 11668
  21.8 7.0 %collective-permute-start.6 = (f32[32,128]{1,0:T(8,128)S(1)}, f32[32,128]{1,0:T(8,128)S(1)}, u32[]{:S(2)}, u32[]{:S(2)}) collective-permute-start(f32[32,128]{1,0:T(8,128)S(1)} %get-tuple-element.53), channel_id=1, source_target_pairs={{0,1},{1,0},{2,3},{3,2},{4,5},{5,4},{6,7},{7,6},{8,9},{9,8},{10,11... | collective-permute-start | bytes 49160 | tf_op jit(solution)/shard_map/ppermute | solution.py:382
  21.9 9.5 %collective-permute-start.7 = (f32[32,128]{1,0:T(8,128)S(1)}, f32[32,128]{1,0:T(8,128)S(1)}, u32[]{:S(2)}, u32[]{:S(2)}) collective-permute-start(f32[32,128]{1,0:T(8,128)S(1)} %get-tuple-element.54), channel_id=1, source_target_pairs={{0,3},{1,2},{2,1},{3,0},{4,7},{5,6},{6,5},{7,4},{8,11},{9,10},{10,... | collective-permute-start | bytes 49160 | tf_op jit(solution)/shard_map/ppermute | solution.py:382
  22.2 9.3 %collective-permute-start.8 = (f32[32,128]{1,0:T(8,128)S(1)}, f32[32,128]{1,0:T(8,128)S(1)}, u32[]{:S(2)}, u32[]{:S(2)}) collective-permute-start(f32[32,128]{1,0:T(8,128)S(1)} %get-tuple-element.55), channel_id=1, source_target_pairs={{0,4},{1,5},{2,6},{3,7},{4,0},{5,1},{6,2},{7,3},{8,12},{9,13},{10,... | collective-permute-start | bytes 49160 | tf_op jit(solution)/shard_map/ppermute | solution.py:382
  28.1 3.4 %collective-permute-start.9 = (f32[32,128]{1,0:T(8,128)S(1)}, f32[32,128]{1,0:T(8,128)S(1)}, u32[]{:S(2)}, u32[]{:S(2)}) collective-permute-start(f32[32,128]{1,0:T(8,128)S(1)} %get-tuple-element.56), channel_id=1, source_target_pairs={{0,1},{1,0},{2,3},{3,2},{4,8},{5,9},{6,10},{7,11},{8,4},{9,5},{10,... | collective-permute-start | bytes 49160 | tf_op jit(solution)/shard_map/ppermute | solution.py:382
  28.1 4.5 %collective-permute-start.10 = (f32[128,128]{1,0:T(8,128)S(1)}, f32[128,128]{1,0:T(8,128)S(1)}, u32[]{:S(2)}, u32[]{:S(2)}) collective-permute-start(f32[128,128]{1,0:T(8,128)S(1)} %get-tuple-element.57), channel_id=1, source_target_pairs={{0,16},{1,17},{2,18},{3,19},{4,20},{5,21},{6,22},{7,23},{8,24},{9,... | collective-permute-start | bytes 196616 | tf_op jit(solution)/shard_map/ppermute | solution.py:382
  28.8 6.4 %collective-permute-start.11 = (f32[128,128]{1,0:T(8,128)S(1)}, f32[128,128]{1,0:T(8,128)S(1)}, u32[]{:S(2)}, u32[]{:S(2)}) collective-permute-start(f32[128,128]{1,0:T(8,128)S(1)} %get-tuple-element.58), channel_id=1, source_target_pairs={{0,1},{1,0},{2,3},{3,2},{4,5},{5,4},{6,7},{7,6},{8,9},{9,8},{10,11... | collective-permute-start | bytes 196616 | tf_op jit(solution)/shard_map/ppermute | solution.py:382

commit v3 on v2

--- a/solution.py
+++ b/solution.py
@@ -16,7 +16,10 @@
 WIDE = 336
 NARROW = PLANE + 4 * NP
 CHUNK = 8
-DEEP = NE * CHUNK
+HALF = 4
+STEPS = -(-NE * NE // CHUNK)
+DEEP = 80
+SIDE = 32
 F32 = jnp.float32
 BF16 = jnp.bfloat16
 
@@ -102,11 +105,15 @@
     flip_second = (code & 2) == 2
     reverse = 7 - lax.broadcasted_iota(jnp.int32, (8, LANES), 0)
 
+    away = from_first | from_second
+    odd_lane = (lanes((8, LANES)) // count) & 1 == 1
+    places = [jnp.where(from_second, position + (block ^ 1) * count, position + block * count) for block in range(blocks)]
+
     def fetch(start):
         block, row = start // rows, start % rows
-        one = lane_take(first_ref[row : row + 8], position + block * count)
-        two = lane_take(second_ref[row : row + 8], position + (block ^ 1) * count)
-        return jnp.where(from_first, one, jnp.where(from_second, two, local(start)))
+        one, two = first_ref[row : row + 8], second_ref[row : row + 8]
+        mixed = jnp.where(odd_lane, one, two) if block % 2 else jnp.where(odd_lane, two, one)
+        return jnp.where(away, lane_take(mixed, places[block]), local(start))
 
     def turn(value):
         return jnp.take_along_axis(value, reverse, axis=0, mode="promise_in_bounds")
@@ -144,16 +151,17 @@
     return plane
 
 
-def pack_kernel(field_ref, table_ref, o0, o1, o2, o3, o4, o5, ids_ref):
+def pack_kernel(field_ref, table_ref, o0, o1, o2, o3, o4, o5, ids_ref, copy_ref):
     outs = (o0, o1, o2, o3, o4, o5)
     start = 0
     for axis in range(3):
         count = LANES * outs[2 * axis].shape[0] // PLANE
-        patterns = block_ids(table_ref[:, start : start + count], odd_place(axis))
+        patterns = block_ids(table_ref[0:2, start : start + count], odd_place(axis))
         start += count
         for half in range(2):
             ids_ref[2 * axis + half : 2 * axis + half + 1] = patterns[half]
         pack_axis(axis, field_plane(field_ref, axis), patterns, count, outs[2 * axis], outs[2 * axis + 1])
+    copy_ref[...] = field_ref[...]
 
 
 def split(value):
@@ -171,56 +179,97 @@
     return jnp.concatenate([high, low, high], axis=1)
 
 
-def exact_dot(a, b):
-    return jnp.dot(a, b, precision=lax.Precision.HIGHEST, preferred_element_type=F32)
-
-
-def write_operators(s_ref, lam_ref, coeff_ref, main_ref, rim_ref, back_ref, to_ref, from_ref, base_ref, edge_ref):
+def parts(value):
+    high = value.astype(BF16)
+    rest = value - high.astype(F32)
+    middle = rest.astype(BF16)
+    return high, middle, (rest - middle.astype(F32)).astype(BF16)
+
+
+def pick_columns(value, hot):
+    return mm(jnp.concatenate(parts(value), axis=1), jnp.concatenate([hot] * 3, axis=0))
+
+
+def pick_rows(hot, value):
+    return mm(jnp.concatenate([hot] * 3, axis=1), jnp.concatenate(parts(value), axis=0))
+
+
+def write_operators(s_ref, lam_ref, coeff_ref, main_ref, rim_ref, back_ref, to_ref, from_ref, ratio_ref, side_ref):
     iota = lambda shape, dim: lax.broadcasted_iota(jnp.int32, shape, dim)
 
     def node(kidx, small_first):
-        inner = kidx < PLANE
-        t = kidx - PLANE
-        group = t // NP
-        along = 1 + t % NP
+        block = kidx >> 4
+        along = 1 + (kidx & (NP - 1))
         if small_first:
-            return jnp.where(inner, 1 + kidx // NP, jnp.where(group == 0, 0, jnp.where(group == 1, NE - 1, along)))
-        return jnp.where(inner, 1 + kidx % NP, jnp.where(group == 2, 0, jnp.where(group == 3, NE - 1, along)))
+            rest = jnp.where(block == NP, 0, jnp.where(block == NP + 1, NE - 1, along))
+            return jnp.where(block < NP, 1 + block, rest)
+        return jnp.where(block == NP + 2, 0, jnp.where(block == NP + 3, NE - 1, along))
+
+    def ones(cond):
+        return jnp.where(cond, 1.0, 0.0).astype(F32)
 
     def hot(cond):
-        return jnp.where(cond, 1.0, 0.0).astype(F32)
-
-    wide_b = hot(iota((WIDE, NE), 0) // NE == iota((WIDE, NE), 1))
-    wide_c = hot((iota((WIDE, NE), 0) % NE == iota((WIDE, NE), 1)) & (iota((WIDE, NE), 0) < NE * NE))
-    wide_bt = hot(iota((NE, WIDE), 1) // NE == iota((NE, WIDE), 0))
-    wide_ct = hot((iota((NE, WIDE), 1) % NE == iota((NE, WIDE), 0)) & (iota((NE, WIDE), 1) < NE * NE))
-    node_j = hot(node(iota((NARROW, NE), 0), True) == iota((NARROW, NE), 1))
-    node_k = hot(node(iota((NARROW, NE), 0), False) == iota((NARROW, NE), 1))
-    node_jt = hot(node(iota((NE, NARROW), 1), True) == iota((NE, NARROW), 0))
-    node_kt = hot(node(iota((NE, NARROW), 1), False) == iota((NE, NARROW), 0))
-    s0, s1, s2 = s_ref[0], s_ref[1], s_ref[2]
+        return ones(cond).astype(BF16)
+
+    def first_of(shape, dim):
+        return (iota(shape, dim) * 3641) >> 16
+
+    def second_of(shape, dim):
+        number = iota(shape, dim)
+        return jnp.where(number < NE * NE, number - NE * first_of(shape, dim), SIDE - 1)
+
+    tall, flat = (WIDE, SIDE), (SIDE, WIDE)
+    nodes, nodes_t = (NARROW, SIDE), (SIDE, NARROW)
+    wide_b = hot(first_of(tall, 0) == iota(tall, 1))
+    wide_c = hot(second_of(tall, 0) == iota(tall, 1))
+    wide_bt = hot(first_of(flat, 1) == iota(flat, 0))
+    wide_ct = hot(second_of(flat, 1) == iota(flat, 0))
+    node_j = hot(node(iota(nodes, 0), True) == iota(nodes, 1))
+    node_k = hot(node(iota(nodes, 0), False) == iota(nodes, 1))
+    node_jt = hot(node(iota(nodes_t, 1), True) == iota(nodes_t, 0))
+    node_kt = hot(node(iota(nodes_t, 1), False) == iota(nodes_t, 0))
+    side_ref[...] = jnp.zeros(side_ref.shape, F32)
+    side_ref[:, :NE, :NE] = s_ref[...]
+    s0, s1, s2 = side_ref[0], side_ref[1], side_ref[2]
     t0, t1, t2 = s0.T, s1.T, s2.T
-    ahead = exact_dot(wide_b, exact_dot(t1, node_jt)) * exact_dot(wide_c, exact_dot(t2, node_kt))
+    ahead = pick_rows(wide_b, pick_columns(t1, node_jt)) * pick_rows(wide_c, pick_columns(t2, node_kt))
     main_ref[...] = operator(ahead[:, :PLANE])
     rim_ref[...] = operator(ahead[:, PLANE:])
-    back = exact_dot(node_j, exact_dot(s1, wide_bt)) * exact_dot(node_k, exact_dot(s2, wide_ct))
+    back = pick_rows(node_j, pick_columns(s1, wide_bt)) * pick_rows(node_k, pick_columns(s2, wide_ct))
     back_ref[...] = operator(back)
-    deep = hot(iota((DEEP, NE), 0) // CHUNK == iota((DEEP, NE), 1))
-    deep_t = hot(iota((NE, DEEP), 1) // CHUNK == iota((NE, DEEP), 0))
-    same = hot(iota((DEEP, DEEP), 0) % CHUNK == iota((DEEP, DEEP), 1) % CHUNK)
-    to_ref[...] = operator(exact_dot(deep, exact_dot(t0, deep_t)) * same)
-    from_ref[...] = operator(exact_dot(deep, exact_dot(s0, deep_t)) * same)
-    col_b = jnp.sum(wide_b * lam_ref[1:2], axis=1, keepdims=True)
-    col_c = jnp.sum(wide_c * lam_ref[2:3], axis=1, keepdims=True)
-    base_ref[...] = col_b * coeff_ref[1:2] + col_c * coeff_ref[2:3]
-    same_a = hot(iota((NE, NE), 0) == iota((NE, NE), 1))
-    edge_ref[...] = jnp.sum(same_a * lam_ref[0:1], axis=1, keepdims=True) * coeff_ref[0:1]
+    deep = hot(iota((DEEP, SIDE), 0) >> 2 == iota((DEEP, SIDE), 1))
+    deep_t = hot(iota((SIDE, DEEP), 1) >> 2 == iota((SIDE, DEEP), 0))
+    same = ones((iota((DEEP, DEEP), 0) ^ iota((DEEP, DEEP), 1)) & (HALF - 1) == 0)
+    to_ref[...] = operator(pick_rows(deep, pick_columns(t0, deep_t)) * same)
+    from_ref[...] = operator(pick_rows(deep, pick_columns(s0, deep_t)) * same)
+    side_ref[0, :3, :NE] = lam_ref[...]
+    lam = [side_ref[0, n : n + 1] for n in range(3)]
+    coeff = [coeff_ref[n : n + 1] for n in range(3)]
+
+    def column(hots, row):
+        return jnp.sum(hots.astype(F32) * row, axis=1, keepdims=True)
+
+    base = column(wide_b, lam[1]) * coeff[1] + column(wide_c, lam[2]) * coeff[2]
+    edge = column(deep, lam[0]) * coeff[0]
+    upper = iota((CHUNK, LANES), 0) < HALF
+    for step in range(STEPS):
+        rows = base[step * CHUNK : (step + 1) * CHUNK]
+        turned = pltpu.roll(rows, HALF, 0)
+        ends = (jnp.where(upper, rows, turned), jnp.where(upper, turned, rows))
+        for s in range(2):
+            for m in range(NE // 2):
+                ratio_ref[step, s, m] = 1.0 / (edge[m * CHUNK : (m + 1) * CHUNK] + ends[s])
 
 
 def mm(a, b):
     return jnp.dot(a, b, preferred_element_type=F32)
 
 
+def table_row(table_ref, number, face):
+    row = 2 + 6 * number + face
+    return table_ref[row : row + 1]
+
+
 def both(load):
     return jnp.concatenate([load(0), load(1)], axis=1)
 
@@ -234,18 +283,16 @@
 
 
 def begin_kernel(
-    field_ref, s_ref, lam_ref, coeff_ref, src_ref, idx_ref, code_ref,
-    main_ref, rim_ref, back_ref, to_ref, from_ref, base_ref, edge_ref, table_ref, local_ref, work_ref,
+    field_ref, table_ref, s_ref, lam_ref, coeff_ref,
+    main_ref, rim_ref, back_ref, to_ref, from_ref, ratio_ref, local_ref, work_ref, side_ref,
 ):
-    for n, ref in enumerate((src_ref, idx_ref, code_ref)):
-        table_ref[n] = ref[...]
-    write_operators(s_ref, lam_ref, coeff_ref, main_ref, rim_ref, back_ref, to_ref, from_ref, base_ref, edge_ref)
+    write_operators(s_ref, lam_ref, coeff_ref, main_ref, rim_ref, back_ref, to_ref, from_ref, ratio_ref, side_ref)
     for face in range(6):
         def put(start, value, face=face):
             local_ref[face * PLANE + start : face * PLANE + start + 8] = value
 
         local_face(
-            face, field_plane(field_ref, face // 2), table_ref[0, face : face + 1], table_ref[1, face : face + 1], put
+            face, field_plane(field_ref, face // 2), table_row(table_ref, 0, face), table_row(table_ref, 1, face), put
         )
     for pair in range(NP // 2):
         got = mm(main_ref[...], stacked(both(lambda s: field_ref[plane_rows(2 * pair + s)])))
@@ -260,13 +307,13 @@
             return local_ref[face * PLANE + start : face * PLANE + start + 8]
 
         axis = face // 2
-        rows = [table_ref[n, face : face + 1] for n in range(3)]
+        rows = [table_row(table_ref, n, face) for n in range(3)]
         result.append(unpack_face(face, local, odd_place(axis), messages[2 * axis], messages[2 * axis + 1], *rows))
     return result
 
 
 def middle_kernel(
-    local_ref, table_ref, ids_ref, first_ref, main_ref, rim_op_ref, back_ref, to_ref, from_ref, base_ref, edge_ref,
+    local_ref, table_ref, ids_ref, first_ref, main_ref, rim_op_ref, back_ref, to_ref, from_ref, ratio_ref,
     m0, m1, m2, m3, m4, m5,
     work_ref, rim_ref, o0, o1, o2, o3, o4, o5,
     ghost_ref,
@@ -288,16 +335,30 @@
             i = 2 * pair + s
             work_ref[1 + i] = first_ref[i] + got[:, s * LANES : (s + 1) * LANES]
 
-    for step in range(WIDE // CHUNK // 2):
-        rows = [slice((2 * step + s) * CHUNK, (2 * step + s + 1) * CHUNK) for s in range(2)]
-        chunk = both(lambda s: work_ref[:, rows[s], :].reshape(DEEP, LANES))
-        coef = mm(to_ref[...], stacked(chunk))
-        divisor = both(
-            lambda s: jnp.concatenate([edge_ref[a : a + 1] + base_ref[rows[s], :] for a in range(NE)], axis=0)
-        )
-        solved = mm(from_ref[...], stacked(coef / divisor))
-        for s in range(2):
-            work_ref[:, rows[s], :] = solved[:, s * LANES : (s + 1) * LANES].reshape(NE, CHUNK, LANES)
+    upper = lax.broadcasted_iota(jnp.int32, (CHUNK, LANES), 0) < HALF
+    swap = lambda value: pltpu.roll(value, HALF, 0)
+    spare = jnp.zeros((DEEP - NE * HALF, LANES), F32)
+    pad = lambda pieces: jnp.concatenate(pieces + [spare], axis=0)
+    for step in range(STEPS):
+        rows = slice(step * CHUNK, (step + 1) * CHUNK)
+        layers = [work_ref[i, rows, :] for i in range(NE)]
+        pairs = list(zip(layers[0::2], layers[1::2]))
+        left = pad([jnp.where(upper, a, swap(b)) for a, b in pairs])
+        right = pad([jnp.where(upper, swap(a), b) for a, b in pairs])
+        coef = mm(to_ref[...], stacked(jnp.concatenate([left, right], axis=1)))
+        scaled = []
+        for s in range(2):
+            pieces = []
+            for m in range(NE // 2):
+                part = slice(m * CHUNK, (m + 1) * CHUNK)
+                pieces.append(coef[part, s * LANES : (s + 1) * LANES] * ratio_ref[step, s, m])
+            scaled.append(pad(pieces))
+        solved = mm(from_ref[...], stacked(jnp.concatenate(scaled, axis=1)))
+        for m in range(NE // 2):
+            part = slice(m * CHUNK, (m + 1) * CHUNK)
+            left, right = solved[part, :LANES], solved[part, LANES:]
+            work_ref[2 * m, rows, :] = jnp.where(upper, left, swap(right))
+            work_ref[2 * m + 1, rows, :] = jnp.where(upper, swap(left), right)
 
     got = mm(back_ref[:PLANE], stacked(both(lambda s: work_ref[s * (NE - 1)])))
     rim_ref[plane_rows(0)] = got[:, :LANES]
@@ -322,7 +383,7 @@
         def put(start, value, face=face):
             local_ref[face * PLANE + start : face * PLANE + start + 8] = value
 
-        local_face(face, rim_plane(rim_ref, face // 2), table_ref[0, face : face + 1], table_ref[1, face : face + 1], put)
+        local_face(face, rim_plane(rim_ref, face // 2), table_row(table_ref, 0, face), table_row(table_ref, 1, face), put)
 
 
 def finish_kernel(inner_ref, local_ref, table_ref, m0, m1, m2, m3, m4, m5, out_hbm, out_ref, sems):
@@ -389,27 +450,29 @@
     shape = jax.ShapeDtypeStruct
     planes = shape((6 * PLANE, LANES), F32)
     block = shape((NP * PLANE, LANES), F32)
+    sends = jnp.concatenate([send_x, send_y, send_z, jnp.zeros((2, 32), jnp.int32)], axis=1)
+    table = jnp.concatenate([sends, nbr_src, nbr_idx, orient], axis=0)
     packed = pl.pallas_call(
-        pack_kernel, out_shape=message_shapes(tables) + [shape((8, LANES), jnp.int32)],
-        in_specs=[VMEM] * 2, out_specs=[VMEM] * 7, compiler_params=grant(8), name="pack",
-    )(flat, jnp.concatenate(tables, axis=1))
-    outgoing, ids = packed[:6], packed[6]
+        pack_kernel, out_shape=message_shapes(tables) + [shape((8, LANES), jnp.int32), block],
+        in_specs=[VMEM] * 2, out_specs=[VMEM] * 8, compiler_params=grant(8), name="pack",
+    )(flat, table)
+    outgoing, (ids, flat) = packed[:6], packed[6:]
     arrived = exchange(outgoing, 0)
     begun = pl.pallas_call(
         begin_kernel,
         out_shape=[
             shape((WIDE, 3 * PLANE), BF16), shape((WIDE, 12 * NP), BF16), shape((NARROW, 3 * WIDE), BF16),
-            shape((DEEP, 3 * DEEP), BF16), shape((DEEP, 3 * DEEP), BF16), shape((WIDE, LANES), F32),
-            shape((NE, LANES), F32), shape((3, 6, LANES), jnp.int32), planes, shape((NP, WIDE, LANES), F32),
+            shape((DEEP, 3 * DEEP), BF16), shape((DEEP, 3 * DEEP), BF16),
+            shape((STEPS, 2, NE // 2, CHUNK, LANES), F32), planes, shape((NP, WIDE, LANES), F32),
         ],
-        in_specs=[VMEM] * 7, out_specs=[VMEM] * 10,
+        in_specs=[VMEM] * 5, out_specs=[VMEM] * 8, scratch_shapes=[pltpu.VMEM((3, SIDE, SIDE), F32)],
         compiler_params=grant(20), name="begin",
         cost_estimate=pl.CostEstimate(flops=2 * 8 * WIDE * 1024 * 256, bytes_accessed=0, transcendentals=0),
-    )(flat, s_mats, lam, coeff, nbr_src, nbr_idx, orient)
-    operators, (table, local, first) = begun[:7], begun[7:]
+    )(flat, table, s_mats, lam, coeff)
+    operators, (local, first) = begun[:6], begun[6:]
     solved = pl.pallas_call(
         middle_kernel, out_shape=[shape((NE, WIDE, LANES), F32), planes] + message_shapes(tables),
-        in_specs=[VMEM] * 17, out_specs=[VMEM] * 8, scratch_shapes=[pltpu.VMEM((6 * PLANE, LANES), F32)],
+        in_specs=[VMEM] * 16, out_specs=[VMEM] * 8, scratch_shapes=[pltpu.VMEM((6 * PLANE, LANES), F32)],
         compiler_params=grant(20), name="middle",
     )(local, table, ids, first, *operators, *arrived)
     work, rims = solved[:2]

time: 37.5 us -> 35.7 us (0.952)
  Pallas kernels: 12.6 us -> 10.8 us
  local copies, waits for them, and re-layouts: 2.38 us -> 1.6 us
  waiting for transfers between devices: 3.72 us -> 4.39 us
    pallas_call x1, Pallas kernels: 4.01 us -> 2.82 us  [shards(): pl.pallas_call(begin_kernel, out_shape=[shape((WIDE, 3 * PLANE), BF16), s...]
    unnamed x16 -> x8, local copies, waits for them, and re-layouts: 2.38 us -> 1.6 us
    ppermute x12, waiting for transfers between devices: 3.72 us -> 4.39 us  [exchange(): arrived[number] = lax.ppermute(messages[number], 'dev', pairs)]
    pallas_call x1, Pallas kernels: 4.63 us -> 4.12 us  [shards(): pl.pallas_call(middle_kernel, out_shape=[shape((NE, WIDE, LANES), F32), p...]
  transfers between devices with their start and end apart: 12 -> 12, of which waited for: 2 -> 3; matrix products, arithmetic and copies ran while one was open for 0% -> 0% of each run, Pallas kernels for 14% -> 12%
where the time goes in v3:
time: 35.7 us; the launch traced here: 35.5 us
  starting transfers between devices  17.6 us (49%)
  Pallas kernels  10.8 us (30%)
  waiting for transfers between devices  4.39 us (12%)
  local copies, waits for them, and re-layouts  1.6 us (4%)
  other arithmetic  0.86 us (2%)
    ppermute x12, starting transfers between devices, exchange(): arrived[number] = lax.ppermute(messages[number], 'dev', pairs)  17.6 us
    ppermute x12, waiting for transfers between devices, exchange(): arrived[number] = lax.ppermute(messages[number], 'dev', pairs)  4.39 us
    pallas_call x1, Pallas kernels, shards(): pl.pallas_call(middle_kernel, out_shape=[shape((NE, WIDE, LANES), F32), p...  4.12 us
    pallas_call x1, Pallas kernels, shards(): pl.pallas_call(begin_kernel, out_shape=[shape((WIDE, 3 * PLANE), BF16), s...  2.82 us
    pallas_call x1, Pallas kernels, shards(): pl.pallas_call(finish_kernel, out_shape=block, in_specs=[VMEM] * 9, out_s...  1.72 us
    unnamed x8, local copies, waits for them, and re-layouts  1.6 us
    pallas_call x1, Pallas kernels, shards(): pl.pallas_call(inside_kernel, out_shape=[block, planes], in_specs=[VMEM]...  1.31 us
    concatenate x1, other arithmetic, shards(): table = jnp.concatenate([sends, nbr_src, nbr_idx, orient], axis=0)  0.86 us
  transfers between devices with their start and end apart: 12, of which 3 were waited for; matrix products, arithmetic and copies ran while one was open for 0% of the time, Pallas kernels for 12%

profile of v3, /device:TPU:2, one launch (start us, length us, event | category | flops | bytes accessed | tf_op | source)
XLA Modules:
  0.0 35.5 jit_solution(1275917438309058796)
XLA Ops:
  0.0 0.9 %pad_add_fusion.table_ref = s32[20,128]{1,0:T(8,128)S(1)} fusion(s32[6,128]{1,0:T(8,128)} %param.16, s32[6,128]{1,0:T(8,128)} %param.15, s32[6,128]{1,0:T(8,128)} %param.14, s32[2,32]{1,0:T(2,128)S(1)} %broadcast_in_dim.3, s32[2,64]{1,0:T(2,128)} %param.19, s32[2,16]{1,0:T(2,128)} %param.18, s32[2,16]{1,0:T(2,128)} %param.17), kind=kLoop, calls=%fused_computation | loop fusion | flops 15360 | bytes 20480 | tf_op jit(solution)/shard_map/concatenate | solution.py:454
  0.9 1.6 %copy-done = f32[16,16,16,128]{3,2,1,0:T(8,128)S(1)} copy-done((f32[16,16,16,128]{3,2,1,0:T(8,128)S(1)}, f32[16,16,16,128]{3,2,1,0:T(8,128)}, u32[]{:S(2)}) %copy-start) | copy-done | bytes 2097176
  2.5 0.8 %pack.1 = (f32[32,128]{1,0:T(8,128)S(1)}, f32[32,128]{1,0:T(8,128)S(1)}, f32[32,128]{1,0:T(8,128)S(1)}, f32[32,128]{1,0:T(8,128)S(1)}, f32[128,128]{1,0:T(8,128)...) custom-call(f32[4096,128]{1,0:T(8,128)S(1)} %bitcast.2, ...), custom_call_target="tpu_custom_call" | custom-call | tf_op jit(solution)/shard_map/pack/pallas_call | solution.py:455
  3.3 0.1 collective-permute-start
  3.4 2.0 %collective-permute-start.1 = (f32[32,128]{1,0:T(8,128)S(1)}, f32[32,128]{1,0:T(8,128)S(1)}, u32[]{:S(2)}, u32[]{:S(2)}) collective-permute-start(f32[32,128]{1,0:T(8,128)S(1)} %get-tuple-element.42), channel_id=1, source_target_pairs={{0,3},{1,2},{2,1},{3,0},{4,7},{5,6},{6,5},{7,4},{8,11},{9,10},{10,... | collective-permute-start | bytes 49160 | tf_op jit(solution)/shard_map/ppermute | solution.py:443
  5.4 3.3 %collective-permute-start.2 = (f32[32,128]{1,0:T(8,128)S(1)}, f32[32,128]{1,0:T(8,128)S(1)}, u32[]{:S(2)}, u32[]{:S(2)}) collective-permute-start(f32[32,128]{1,0:T(8,128)S(1)} %get-tuple-element.43), channel_id=1, source_target_pairs={{0,4},{1,5},{2,6},{3,7},{4,0},{5,1},{6,2},{7,3},{8,12},{9,13},{10,... | collective-permute-start | bytes 49160 | tf_op jit(solution)/shard_map/ppermute | solution.py:443
  8.7 0.0 collective-permute-start.3
  8.7 1.6 %collective-permute-start.4 = (f32[128,128]{1,0:T(8,128)S(1)}, f32[128,128]{1,0:T(8,128)S(1)}, u32[]{:S(2)}, u32[]{:S(2)}) collective-permute-start(f32[128,128]{1,0:T(8,128)S(1)} %get-tuple-element.45), channel_id=1, source_target_pairs={{0,16},{1,17},{2,18},{3,19},{4,20},{5,21},{6,22},{7,23},{8,24},{9,... | collective-permute-start | bytes 196616 | tf_op jit(solution)/shard_map/ppermute | solution.py:443
  10.2 2.2 %collective-permute-start.5 = (f32[128,128]{1,0:T(8,128)S(1)}, f32[128,128]{1,0:T(8,128)S(1)}, u32[]{:S(2)}, u32[]{:S(2)}) collective-permute-start(f32[128,128]{1,0:T(8,128)S(1)} %get-tuple-element.46), channel_id=1, source_target_pairs={{0,1},{1,0},{2,3},{3,2},{4,5},{5,4},{6,7},{7,6},{8,9},{9,8},{10,11... | collective-permute-start | bytes 196616 | tf_op jit(solution)/shard_map/ppermute | solution.py:443
  12.4 2.8 %begin.1 = (bf16[336,768]{1,0:T(8,128)(2,1)S(1)}, bf16[336,192]{1,0:T(8,128)(2,1)S(1)}, bf16[320,1008]{1,0:T(8,128)(2,1)S(1)}, bf16[80,240]{1,0:T(8,128)(2,1)S(1...) custom-call(f32[4096,128]{1,0:T(8,128)S(1)} %get-tuple-element.31.fi, ...), custom_call_target="tpu_custom_call" | custom-call | flops 1409286144 | tf_op jit(solution)/shard_map/begin/pallas_call | solution.py:461
  15.2 0.0 collective-permute-done.2.m2
  15.3 1.3 %collective-permute-done.5.m5 = f32[128,128]{1,0:T(8,128)S(1)} collective-permute-done((f32[128,128]{1,0:T(8,128)S(1)}, f32[128,128]{1,0:T(8,128)S(1)}, u32[]{:S(2)}, u32[]{:S(2)}) %collective-permute-start.5) | collective-permute-done | bytes 65568 | tf_op jit(solution)/shard_map/ppermute | solution.py:443
  16.6 4.1 %middle.1 = (f32[18,336,128]{2,1,0:T(8,128)S(1)}, f32[1536,128]{1,0:T(8,128)S(1)}, f32[32,128]{1,0:T(8,128)S(1)}, f32[32,128]{1,0:T(8,128)S(1)}, f32[32,128]{1,0...) custom-call(f32[1536,128]{1,0:T(8,128)S(1)} %get-tuple-element.32.local_ref, ...), custom_call_target="tpu_custom_call" | custom-call | tf_op jit(solution)/shard_map/middle/pallas_call | solution.py:473
  20.7 0.1 collective-permute-start.6
  20.8 0.2 collective-permute-start.7
  21.1 6.0 %collective-permute-start.8 = (f32[32,128]{1,0:T(8,128)S(1)}, f32[32,128]{1,0:T(8,128)S(1)}, u32[]{:S(2)}, u32[]{:S(2)}) collective-permute-start(f32[32,128]{1,0:T(8,128)S(1)} %get-tuple-element.53), channel_id=1, source_target_pairs={{0,4},{1,5},{2,6},{3,7},{4,0},{5,1},{6,2},{7,3},{8,12},{9,13},{10,... | collective-permute-start | bytes 49160 | tf_op jit(solution)/shard_map/ppermute | solution.py:443
  27.0 0.0 collective-permute-start.10
  27.0 2.2 %collective-permute-start.11 = (f32[128,128]{1,0:T(8,128)S(1)}, f32[128,128]{1,0:T(8,128)S(1)}, u32[]{:S(2)}, u32[]{:S(2)}) collective-permute-start(f32[128,128]{1,0:T(8,128)S(1)} %get-tuple-element.56), channel_id=1, source_target_pairs={{0,1},{1,0},{2,3},{3,2},{4,5},{5,4},{6,7},{7,6},{8,9},{9,8},{10,11... | collective-permute-start | bytes 196616 | tf_op jit(solution)/shard_map/ppermute | solution.py:443
  29.3 1.3 %inside.1 = (f32[4096,128]{1,0:T(8,128)S(1)}, f32[1536,128]{1,0:T(8,128)S(1)}) custom-call(f32[18,336,128]{2,1,0:T(8,128)S(1)} %get-tuple-element.47.work_ref, bf16[320,1008]{1,0:T(8,128)(2,1)S(1)} %get-tuple-element.37.back_ref, f32[1536,128]{1,0:T(8,128)S(1)} %get-tuple-element.48.rim_ref, s32[20,128]{1,0:T(8,128)S(1)} %pad_add_fusion.table_ref), custom_call_target="tpu_custom_call" | custom-call | flops 1073741824 | tf_op jit(solution)/shard_map/inside/pallas_call | solution.py:480
  30.6 0.0 collective-permute-done.7.m1
  30.6 0.0 collective-permute-done.9.m3
  30.6 0.9 %collective-permute-done.10.m4 = f32[128,128]{1,0:T(8,128)S(1)} collective-permute-done((f32[128,128]{1,0:T(8,128)S(1)}, f32[128,128]{1,0:T(8,128)S(1)}, u32[]{:S(2)}, u32[]{:S(2)}) %collective-permute-start.10) | collective-permute-done | bytes 65568 | tf_op jit(solution)/shard_map/ppermute | solution.py:443
  31.5 2.1 %collective-permute-done.11.m5 = f32[128,128]{1,0:T(8,128)S(1)} collective-permute-done((f32[128,128]{1,0:T(8,128)S(1)}, f32[128,128]{1,0:T(8,128)S(1)}, u32[]{:S(2)}, u32[]{:S(2)}) %collective-permute-start.11) | collective-permute-done | bytes 65568 | tf_op jit(solution)/shard_map/ppermute | solution.py:443
  33.6 1.7 %finish.1 = f32[4096,128]{1,0:T(8,128)} custom-call(f32[4096,128]{1,0:T(8,128)S(1)} %get-tuple-element.49.inner_ref, f32[1536,128]{1,0:T(8,128)S(1)} %get-tuple-element.50.local_ref, s32[20,128]{1,0:T(8,128)S(1)} %pad_add_fusion.table_ref, f32[32,128]{1,0:T(8,128)S(1)} %collective-permute-done.6.m0, f32[32,128]{1,0:T(8,128)S(1)} %collective-permute-done.7.m1, ...), custom_call_target="tpu_custom_call" | custom-call | tf_op jit(solution)/shard_map/finish/pallas_call | solution.py:485
  (15 shorter events, 0.0 us)
Async XLA Ops:
  0.0 12.4 %copy-start.3 = (f32[3,128]{1,0:T(4,128)S(1)}, f32[3,128]{1,0:T(4,128)}, u32[]{:S(2)}) copy-start(f32[3,128]{1,0:T(4,128)} %coeff_ref.1) | copy-start | bytes 4612
  0.0 12.4 %copy-start.2 = (f32[3,18]{1,0:T(4,128)S(1)}, f32[3,18]{1,0:T(4,128)}, u32[]{:S(2)}) copy-start(f32[3,18]{1,0:T(4,128)} %lam_ref.1) | copy-start | bytes 652
  0.9 1.6 %copy-start = (f32[16,16,16,128]{3,2,1,0:T(8,128)S(1)}, f32[16,16,16,128]{3,2,1,0:T(8,128)}, u32[]{:S(2)}) copy-start(f32[16,16,16,128]{3,2,1,0:T(8,128)} %param.10) | copy-start | bytes 6291460
  2.5 9.9 %copy-start.1 = (f32[3,18,18]{2,1,0:T(8,128)S(1)}, f32[3,18,18]{2,1,0:T(8,128)}, u32[]{:S(2)}) copy-start(f32[3,18,18]{2,1,0:T(8,128)} %s_ref.1) | copy-start | bytes 11668
  3.3 7.0 %collective-permute-start = (f32[32,128]{1,0:T(8,128)S(1)}, f32[32,128]{1,0:T(8,128)S(1)}, u32[]{:S(2)}, u32[]{:S(2)}) collective-permute-start(f32[32,128]{1,0:T(8,128)S(1)} %get-tuple-element.41), channel_id=1, source_target_pairs={{0,1},{1,0},{2,3},{3,2},{4,5},{5,4},{6,7},{7,6},{8,9},{9,8},{10,11... | collective-permute-start | bytes 49160 | tf_op jit(solution)/shard_map/ppermute | solution.py:443
  3.4 11.9 %collective-permute-start.1 = (f32[32,128]{1,0:T(8,128)S(1)}, f32[32,128]{1,0:T(8,128)S(1)}, u32[]{:S(2)}, u32[]{:S(2)}) collective-permute-start(f32[32,128]{1,0:T(8,128)S(1)} %get-tuple-element.42), channel_id=1, source_target_pairs={{0,3},{1,2},{2,1},{3,0},{4,7},{5,6},{6,5},{7,4},{8,11},{9,10},{10,... | collective-permute-start | bytes 49160 | tf_op jit(solution)/shard_map/ppermute | solution.py:443
  5.4 9.9 %collective-permute-start.2 = (f32[32,128]{1,0:T(8,128)S(1)}, f32[32,128]{1,0:T(8,128)S(1)}, u32[]{:S(2)}, u32[]{:S(2)}) collective-permute-start(f32[32,128]{1,0:T(8,128)S(1)} %get-tuple-element.43), channel_id=1, source_target_pairs={{0,4},{1,5},{2,6},{3,7},{4,0},{5,1},{6,2},{7,3},{8,12},{9,13},{10,... | collective-permute-start | bytes 49160 | tf_op jit(solution)/shard_map/ppermute | solution.py:443
  8.7 6.6 %collective-permute-start.3 = (f32[32,128]{1,0:T(8,128)S(1)}, f32[32,128]{1,0:T(8,128)S(1)}, u32[]{:S(2)}, u32[]{:S(2)}) collective-permute-start(f32[32,128]{1,0:T(8,128)S(1)} %get-tuple-element.44), channel_id=1, source_target_pairs={{0,1},{1,0},{2,3},{3,2},{4,8},{5,9},{6,10},{7,11},{8,4},{9,5},{10,... | collective-permute-start | bytes 49160 | tf_op jit(solution)/shard_map/ppermute | solution.py:443
  8.7 6.6 %collective-permute-start.4 = (f32[128,128]{1,0:T(8,128)S(1)}, f32[128,128]{1,0:T(8,128)S(1)}, u32[]{:S(2)}, u32[]{:S(2)}) collective-permute-start(f32[128,128]{1,0:T(8,128)S(1)} %get-tuple-element.45), channel_id=1, source_target_pairs={{0,16},{1,17},{2,18},{3,19},{4,20},{5,21},{6,22},{7,23},{8,24},{9,... | collective-permute-start | bytes 196616 | tf_op jit(solution)/shard_map/ppermute | solution.py:443
  10.2 6.4 %collective-permute-start.5 = (f32[128,128]{1,0:T(8,128)S(1)}, f32[128,128]{1,0:T(8,128)S(1)}, u32[]{:S(2)}, u32[]{:S(2)}) collective-permute-start(f32[128,128]{1,0:T(8,128)S(1)} %get-tuple-element.46), channel_id=1, source_target_pairs={{0,1},{1,0},{2,3},{3,2},{4,5},{5,4},{6,7},{7,6},{8,9},{9,8},{10,11... | collective-permute-start | bytes 196616 | tf_op jit(solution)/shard_map/ppermute | solution.py:443
  20.7 6.3 %collective-permute-start.6 = (f32[32,128]{1,0:T(8,128)S(1)}, f32[32,128]{1,0:T(8,128)S(1)}, u32[]{:S(2)}, u32[]{:S(2)}) collective-permute-start(f32[32,128]{1,0:T(8,128)S(1)} %get-tuple-element.51), channel_id=1, source_target_pairs={{0,1},{1,0},{2,3},{3,2},{4,5},{5,4},{6,7},{7,6},{8,9},{9,8},{10,11... | collective-permute-start | bytes 49160 | tf_op jit(solution)/shard_map/ppermute | solution.py:443
  20.8 9.7 %collective-permute-start.7 = (f32[32,128]{1,0:T(8,128)S(1)}, f32[32,128]{1,0:T(8,128)S(1)}, u32[]{:S(2)}, u32[]{:S(2)}) collective-permute-start(f32[32,128]{1,0:T(8,128)S(1)} %get-tuple-element.52), channel_id=1, source_target_pairs={{0,3},{1,2},{2,1},{3,0},{4,7},{5,6},{6,5},{7,4},{8,11},{9,10},{10,... | collective-permute-start | bytes 49160 | tf_op jit(solution)/shard_map/ppermute | solution.py:443
  21.1 9.5 %collective-permute-start.8 = (f32[32,128]{1,0:T(8,128)S(1)}, f32[32,128]{1,0:T(8,128)S(1)}, u32[]{:S(2)}, u32[]{:S(2)}) collective-permute-start(f32[32,128]{1,0:T(8,128)S(1)} %get-tuple-element.53), channel_id=1, source_target_pairs={{0,4},{1,5},{2,6},{3,7},{4,0},{5,1},{6,2},{7,3},{8,12},{9,13},{10,... | collective-permute-start | bytes 49160 | tf_op jit(solution)/shard_map/ppermute | solution.py:443
  27.0 3.6 %collective-permute-start.9 = (f32[32,128]{1,0:T(8,128)S(1)}, f32[32,128]{1,0:T(8,128)S(1)}, u32[]{:S(2)}, u32[]{:S(2)}) collective-permute-start(f32[32,128]{1,0:T(8,128)S(1)} %get-tuple-element.54), channel_id=1, source_target_pairs={{0,1},{1,0},{2,3},{3,2},{4,8},{5,9},{6,10},{7,11},{8,4},{9,5},{10,... | collective-permute-start | bytes 49160 | tf_op jit(solution)/shard_map/ppermute | solution.py:443
  27.0 4.5 %collective-permute-start.10 = (f32[128,128]{1,0:T(8,128)S(1)}, f32[128,128]{1,0:T(8,128)S(1)}, u32[]{:S(2)}, u32[]{:S(2)}) collective-permute-start(f32[128,128]{1,0:T(8,128)S(1)} %get-tuple-element.55), channel_id=1, source_target_pairs={{0,16},{1,17},{2,18},{3,19},{4,20},{5,21},{6,22},{7,23},{8,24},{9,... | collective-permute-start | bytes 196616 | tf_op jit(solution)/shard_map/ppermute | solution.py:443
  27.0 6.6 %collective-permute-start.11 = (f32[128,128]{1,0:T(8,128)S(1)}, f32[128,128]{1,0:T(8,128)S(1)}, u32[]{:S(2)}, u32[]{:S(2)}) collective-permute-start(f32[128,128]{1,0:T(8,128)S(1)} %get-tuple-element.56), channel_id=1, source_target_pairs={{0,1},{1,0},{2,3},{3,2},{4,5},{5,4},{6,7},{7,6},{8,9},{9,8},{10,11... | collective-permute-start | bytes 196616 | tf_op jit(solution)/shard_map/ppermute | solution.py:443
